TPU v7x, 256 devices: a whole 4x4x8 slice. The times are simulated.
256 devices in a mesh: dp: 32 (over y, z), neg: 8 (over x, core).
Axes of the slice: x: 4, y: 4, z: 8, core: 2. Of those that a mesh axis runs over, the one named last changes fastest.
Arguments:
- query_features: bfloat16 [65536, 512], P(('dp', 'neg')), may hold values from -8 to 8
- positive_features: bfloat16 [65536, 512], P(('dp', 'neg')), may hold values from -6 to 6
- negative_features: bfloat16 [16384, 512], P(('neg', 'dp')), may hold values from -6 to 6
- positive_ids: int32 [65536], P('dp'), may hold values from 0 to 8191, as said below
- positive_counts: int32 [65536], P(('dp', 'neg')), may hold values from 1 to 16
- negative_ids: int32 [16384], P('neg'), may hold values from 0 to 4095, as said below
- negative_counts: int32 [16384], P('neg'), may hold values from 64 to 4096
- query_first: bfloat16 [512, 1024], replicated, may hold values from -0.25 to 0.25
- query_second: bfloat16 [1024, 512], replicated, may hold values from -0.1875 to 0.1875
- query_third: bfloat16 [512, 256], replicated, may hold values from -0.25 to 0.25
- item_first: bfloat16 [512, 1024], replicated, may hold values from -0.25 to 0.25
- item_second: bfloat16 [1024, 512], replicated, may hold values from -0.1875 to 0.1875
- item_third: bfloat16 [512, 256], replicated, may hold values from -0.25 to 0.25
Outputs:
- mean_loss: float32 [], replicated
- clipped_query_first: float32 [512, 1024], P('dp')
- clipped_query_second: float32 [1024, 512], P('dp')
- clipped_query_third: float32 [512, 256], P('dp')
- clipped_item_first: float32 [512, 1024], P('dp')
- clipped_item_second: float32 [1024, 512], P('dp')
- clipped_item_third: float32 [512, 256], P('dp')
Inputs may be any that keep to these rules, and one draw needn't show every extreme that they name: `negative_ids`: ids of the sampled negatives; one id may stand for several negatives. `positive_ids`: A query's positive id may equal the ids of some negatives; those negatives are left out of that query's denominator.
All inputs are finite; a program needn't handle non-finite values.
Results may differ from a plain program's by a relative error of at most 0.0075.
Values may be sent and summed in bfloat16 or wider, within the bound.
A program may use at most 128 MiB of HBM per device.

v0:
```python
import jax
import jax.numpy as jnp
from jax import lax
from jax.sharding import Mesh
from jax.sharding import PartitionSpec as P

NEG = ("neg_0", "neg_1")
DP = ("dp_0", "dp_1")
DP_NEG = ("dp_0", "dp_1", "neg_0", "neg_1")
NEG_DP = ("neg_0", "neg_1", "dp_0", "dp_1")


inv_temp = 20.0
clip_norm = 256.0


def laid_out(tiles, dim):
    tiles = jnp.moveaxis(tiles, 0, dim)
    shape = tiles.shape
    return tiles.reshape(*shape[:dim], shape[dim] * shape[dim + 1], *shape[dim + 2 :])


def from_everyone(array, axis):
    copies = jnp.broadcast_to(array, (lax.axis_size(axis), *array.shape))
    return lax.all_to_all(copies, axis, split_axis=0, concat_axis=0, tiled=True)


def collect(array, axis, dim):
    return laid_out(from_everyone(array, axis), dim)


def over_copies(array, axis):
    return from_everyone(array, axis).sum(axis=0)


def cut_along(array, dim, length):
    shape = array.shape
    tiles = array.reshape(*shape[:dim], length, shape[dim] // length, *shape[dim + 1 :])
    return jnp.moveaxis(tiles, dim, 0)


def sent_and_summed(array, axis, dim):
    length = lax.axis_size(axis)
    tiles = lax.all_to_all(cut_along(array, dim, length), axis, 0, 0, tiled=True)
    return jnp.sum(tiles, axis=0)


def own_rows_2(so_far, axes):
    for axis in axes:
        so_far = lax.psum_scatter(so_far, axis, scatter_dimension=0, tiled=True)
    return so_far


def by_axis(array, axes):
    for axis in axes:
        array = lax.psum(array, axis)
    return array


def one_scatter(arrays, axis, dims):
    length = lax.axis_size(axis)
    tiles = [cut_along(a, dim, length) for a, dim in zip(arrays, dims)]
    lines = jnp.concatenate([b.reshape(length, -1) for b in tiles], axis=1)
    width = max(16, -(-lines.shape[1] // 1024) * 8)
    lines = jnp.pad(lines, ((0, 0), (0, width * 128 - lines.shape[1]))).reshape(-1, 128)
    vector, at, finished = (lax.psum_scatter(lines, axis, tiled=True).reshape(-1), 0, [])
    for b in tiles:
        part = b[0]
        finished.append(vector[at : at + part.size].reshape(part.shape))
        at += part.size
    return tuple(finished)


def gather_together(arrays, axis, dims):
    vector = jnp.concatenate([a.reshape(-1) for a in arrays])
    lines, at, finished = (lax.all_gather(vector, axis), 0, [])
    for a, dim in zip(arrays, dims):
        tiles = lines[:, at : at + a.size].reshape(-1, *a.shape)
        finished.append(laid_out(tiles, dim))
        at += a.size
    return tuple(finished)


def silu_slope(pre):
    sigma = jax.nn.sigmoid(pre)
    return sigma * (1.0 + pre * (1.0 - sigma))


def contract_rows(left, right):
    return lax.dot_general(
        left, right, (((0,), (0,)), ((), ())), preferred_element_type=jnp.float32
    )


def contract_cols(left, right):
    return lax.dot_general(
        left, right, (((1,), (1,)), ((), ())), preferred_element_type=jnp.float32
    )


def tower_forward(features, first, second, third):
    first_pre = jnp.dot(features, first, preferred_element_type=jnp.float32)
    first_act = jax.nn.silu(first_pre).astype(jnp.bfloat16)
    second_pre = jnp.dot(first_act, second, preferred_element_type=jnp.float32)
    second_act = jax.nn.silu(second_pre).astype(jnp.bfloat16)
    embedding = jnp.dot(second_act, third, preferred_element_type=jnp.float32)
    inv_norm = lax.rsqrt(jnp.sum(embedding * embedding, axis=1, keepdims=True) + 1.0)
    unit = (embedding * inv_norm).astype(jnp.bfloat16)
    return ((first_pre, first_act, second_pre, second_act, embedding, inv_norm), unit)


def tower_backward(features, second, third, saved, unit_grad):
    first_pre, first_act, second_pre, second_act, embedding, inv_norm = saved
    along = jnp.sum(embedding * unit_grad, axis=1, keepdims=True)
    embed_grad = (inv_norm * unit_grad - inv_norm * inv_norm * inv_norm * embedding * along).astype(
        jnp.bfloat16
    )
    third_grad = contract_rows(second_act, embed_grad)
    second_slope = (contract_cols(embed_grad, third) * silu_slope(second_pre)).astype(jnp.bfloat16)
    second_grad = contract_rows(first_act, second_slope)
    first_slope = (contract_cols(second_slope, second) * silu_slope(first_pre)).astype(jnp.bfloat16)
    first_grad = contract_rows(features, first_slope)
    return (first_grad, second_grad, third_grad)


def per_device(
    query_features,
    positive_features,
    negative_features,
    positive_ids,
    positive_counts,
    negative_ids,
    negative_counts,
    query_first,
    query_second,
    query_third,
    item_first,
    item_second,
    item_third,
):
    own_rows = query_features.shape[0]
    query_saved, query_unit = tower_forward(query_features, query_first, query_second, query_third)
    item_features = jnp.concatenate([positive_features, negative_features], axis=0)
    item_saved, item_unit = tower_forward(item_features, item_first, item_second, item_third)
    positive_unit = item_unit[:own_rows]
    negative_unit = item_unit[own_rows:]
    group_unit = collect(query_unit, NEG, 0)
    shard_unit = collect(negative_unit, DP, 0)
    scores = (
        contract_cols(group_unit, shard_unit) * inv_temp
        - jnp.log(negative_counts.astype(jnp.float32))[None, :]
    )
    weights = jnp.where(positive_ids[:, None] != negative_ids[None, :], jnp.exp(scores), 0.0)
    positive_logit = jnp.sum(
        query_unit.astype(jnp.float32) * positive_unit.astype(jnp.float32), axis=1
    ) * inv_temp - jnp.log(positive_counts.astype(jnp.float32))
    positive_exp = jnp.exp(positive_logit)
    offset = lax.axis_index(NEG) * own_rows
    partial_value = jnp.sum(weights, axis=1)
    own_part = lax.dynamic_slice(partial_value, (offset,), (own_rows,)) + positive_exp
    partial_value = lax.dynamic_update_slice(partial_value, own_part, (offset,))
    denom = over_copies(partial_value, NEG)
    own_denom = lax.dynamic_slice(denom, (offset,), (own_rows,))
    loss_part = jnp.sum(jnp.log(own_denom) - positive_logit)
    softmax_weights = (weights / denom[:, None]).astype(jnp.bfloat16)
    positive_slope = positive_exp / own_denom - 1.0
    block = softmax_weights
    query_sum = sent_and_summed(
        jnp.dot(block, shard_unit, preferred_element_type=jnp.float32), NEG, 0
    )
    query_grad = (
        query_sum + positive_slope[:, None] * positive_unit.astype(jnp.float32)
    ) * inv_temp
    block = softmax_weights
    negative_sum = own_rows_2(contract_rows(block, group_unit), DP)
    positive_grad = positive_slope[:, None] * query_unit.astype(jnp.float32) * inv_temp
    item_grad = jnp.concatenate([positive_grad, negative_sum * inv_temp], axis=0)
    query_grads = tower_backward(query_features, query_second, query_third, query_saved, query_grad)
    item_grads = tower_backward(item_features, item_second, item_third, item_saved, item_grad)
    gradients = query_grads + item_grads
    loss_sum = by_axis(loss_part, DP_NEG)
    mean_loss = loss_sum / (own_rows * lax.axis_size(DP) * lax.axis_size(NEG))
    vectors = tuple((gradient.reshape(-1) for gradient in gradients))
    pieces = one_scatter(
        (vectors[0], vectors[1], vectors[2], vectors[3], vectors[4], vectors[5]),
        DP_NEG,
        (0, 0, 0, 0, 0, 0),
    )
    squares = jnp.zeros((), jnp.float32)
    for piece in pieces:
        squares = squares + jnp.sum(piece * piece)
    grad_norm = jnp.sqrt(by_axis(squares, DP_NEG))
    clip_factor = clip_norm / jnp.maximum(grad_norm, clip_norm)
    scaled = tuple((piece * clip_factor for piece in pieces))
    gathered = gather_together(
        (scaled[0], scaled[1], scaled[2], scaled[3], scaled[4], scaled[5]), NEG, (0, 0, 0, 0, 0, 0)
    )
    clipped = tuple(
        (vector.reshape(-1, gradient.shape[1]) for vector, gradient in zip(gathered, gradients))
    )
    return (mean_loss, clipped[0], clipped[1], clipped[2], clipped[3], clipped[4], clipped[5])


def solution(mesh):
    torus = Mesh(mesh.devices.reshape(4, 8, 4, 2), ("dp_0", "dp_1", "neg_0", "neg_1"))
    placed = (
        P(DP_NEG, None),
        P(DP_NEG, None),
        P(NEG_DP, None),
        P(DP),
        P(DP_NEG),
        P(NEG),
        P(NEG),
        P(),
        P(),
        P(),
        P(),
        P(),
        P(),
    )
    return jax.shard_map(
        per_device,
        mesh=torus,
        in_specs=placed,
        out_specs=(
            P(),
            P(DP, None),
            P(DP, None),
            P(DP, None),
            P(DP, None),
            P(DP, None),
            P(DP, None),
        ),
        check_vma=False,
    )
```

profile of v0, /device:TPU:1, one launch (start us, length us, event | category | flops | bytes accessed | tf_op | source)
XLA Modules:
  0.0 581.6 jit_solution(1394831791361517272)
XLA Ops:
  7.2 1.1 constant_dynamic-update-slice_fusion.1
  8.3 0.8 constant_dynamic-update-slice_fusion
  9.2 0.7 copy-done.11
  9.9 1.7 fusion.24
  11.7 1.4 multiply_convert_fusion.2
  14.0 1.3 multiply_convert_fusion.3
  16.5 1.1 broadcast_in_dim.10
  17.6 6.7 %all-to-all-start = ((bf16[8,256,256]{2,1,0:T(8,128)(2,1)}), bf16[8,256,256]{2,1,0:T(8,128)(2,1)S(1)}, u32[]{:S(2)}, u32[]{:S(2)}) async-start(bf16[8,256,256]{2,1,0:T(8,128)(2,1)} %broadcast_in_dim.10), calls=%async_computation | async-start | bytes 2097152 | tf_op jit(solution)/shard_map/all_to_all | solution.py:25
  24.2 15.0 %all-to-all-done = bf16[8,256,256]{2,1,0:T(8,128)(2,1)S(1)} async-done(((bf16[8,256,256]{2,1,0:T(8,128)(2,1)}), bf16[8,256,256]{2,1,0:T(8,128)(2,1)S(1)}, u32[]{:S(2)}, u32[]{:S(2)}) %all-to-all-start) | async-done | bytes 1048608 | tf_op jit(solution)/shard_map/all_to_all | solution.py:25
  39.2 1.1 broadcast_in_dim.11
  40.3 10.4 %all-to-all-start.1 = ((bf16[32,64,256]{2,1,0:T(8,128)(2,1)}), bf16[32,64,256]{2,1,0:T(8,128)(2,1)}, u32[]{:S(2)}, u32[]{:S(2)}) async-start(bf16[32,64,256]{2,1,0:T(8,128)(2,1)} %broadcast_in_dim.11), calls=%async_computation.1 | async-start | bytes 2097152 | tf_op jit(solution)/shard_map/all_to_all | solution.py:25
  50.8 25.0 %all-to-all-done.1 = bf16[32,64,256]{2,1,0:T(8,128)(2,1)} async-done(((bf16[32,64,256]{2,1,0:T(8,128)(2,1)}), bf16[32,64,256]{2,1,0:T(8,128)(2,1)}, u32[]{:S(2)}, u32[]{:S(2)}) %all-to-all-start.1) | async-done | bytes 1048608 | tf_op jit(solution)/shard_map/all_to_all | solution.py:25
  75.9 9.2 %fusion = (f32[2048]{0:T(1024)S(1)}, f32[2048,2048]{1,0:T(8,128)}) fusion(f32[2048]{0:T(1024)S(1)} %convert_log_fusion, s32[2048]{0:T(1024)S(1)} %copy-done.22, s32[2048]{0:T(1024)S(1)} %copy-done.23, bf16[2048,256]{1,0:T(8,128)(2,1)S(1)} %bitcast.52, bf16[2048,256]{1,0:T(8,128)(2,1)} %bitcast.1), kind=kOutput, calls=%fused_computation.2 | convolution fusion | flops 2168453120 | bytes 18907136 | tf_op jit(solution)/shard_map/dot_general | solution.py:96
  85.3 11.9 %all_to_all.21 = f32[8,1,2048]{2,1,0:T(1,128)S(1)} all-to-all(f32[8,1,2048]{2,1,0:T(1,128)S(1)} %broadcast_in_dim.13), channel_id=1, replica_groups=mesh['dp_0'=4,'dp_1'=8,'neg_0'=4,'neg_1'=2] {'neg_0','neg_1'}, dimensions={0} | all-to-all | bytes 131072 | tf_op jit(solution)/shard_map/all_to_all | solution.py:25
  97.2 8.4 %divide_convert_fusion = bf16[2048,2048]{1,0:T(8,128)(2,1)S(1)} fusion(f32[2048,2048]{1,0:T(8,128)} %get-tuple-element.47, f32[2048]{0:T(1024)S(1)} %reduce_sum.139, f32[2048]{0:T(1024)S(1)} %convert_log_fusion, s32[2048]{0:T(1024)S(1)} %copy-done.22, s32[2048]{0:T(1024)S(1)} %copy-done.23), kind=kLoop, calls=%fused_computation | loop fusion | flops 25165824 | bytes 25198592 | tf_op jit(solution)/shard_map/convert_element_type | solution.py:165
  105.7 3.2 copy-done.1
  108.9 3.9 fusion.27
  112.8 7.3 %fusion.25 = f32[8,256,256]{2,1,0:T(8,128)} fusion(bf16[8,256,2048]{2,1,0:T(8,128)(2,1)} %bitcast.51, bf16[2048,256,1]{1,0,2:T(8,128)(2,1)} %bitcast.3), kind=kOutput, calls=%fused_computation.85 | convolution fusion | flops 2147483648 | bytes 11534336 | tf_op jit(solution)/shard_map/dot_general | solution.py:169
  120.1 4.3 all-to-all-start.3
  124.3 0.7 divide_add_fusion
  125.0 25.5 %all-to-all-done.3 = f32[8,256,256]{2,1,0:T(8,128)S(1)} async-done(((f32[8,256,256]{2,1,0:T(8,128)}), f32[8,256,256]{2,1,0:T(8,128)S(1)}, u32[]{:S(2)}, u32[]{:S(2)}) %all-to-all-start.3) | async-done | bytes 2097184 | tf_op jit(solution)/shard_map/all_to_all | solution.py:44
  150.6 0.9 reduce_sum.141
  151.4 2.0 fusion.12
  153.4 1.3 subtract_convert_fusion.1
  155.3 2.2 fusion.5
  157.5 2.6 convolution_bitcast_fusion
  160.4 3.1 fusion.17
  163.5 1.8 copy.24
  165.3 1.9 reshape_reshape.36
  167.2 3.2 reshape_reshape.37
  170.4 2.1 fusion.26
  172.5 2.0 reshape_reshape.38
  174.5 1.5 constant_dynamic-update-slice_fusion.7
  175.9 3.3 constant_dynamic-update-slice_fusion.6
  179.2 0.9 constant_dynamic-update-slice_fusion.5
  180.1 7.9 %reduce-scatter.5.cloned.1.call-done = f32[64,256]{1,0:T(8,128)} async-done(((f32[512,256]{1,0:T(8,128)}), f32[64,256]{1,0:T(8,128)}) %reduce-scatter.5.cloned.1.call-update) | async-done | bytes 65552 | tf_op jit(solution)/shard_map/reduce_scatter | solution.py:50
  188.0 0.8 broadcast_multiply_fusion
  188.9 1.1 multiply_reduce_fusion
  190.0 1.1 subtract_convert_fusion
  191.8 1.5 fusion.4
  193.4 2.5 fusion.2
  195.9 2.2 fusion.19
  198.1 1.1 fusion.28
  199.2 1.9 reshape_reshape.39
  201.1 3.2 reshape_reshape.40
  204.3 2.0 reshape_reshape.41
  206.3 1.6 constant_dynamic-update-slice_fusion.4
  207.8 3.2 constant_dynamic-update-slice_fusion.3
  211.0 0.8 constant_dynamic-update-slice_fusion.2
  211.9 9.9 %reshape.88 = f32[18432,128]{1,0:T(8,128)} reshape(f32[256,9216]{1,0:T(8,128)} %constant_dynamic-update-slice_fusion.2) | data formatting | bytes 18874368 | tf_op jit(solution)/shard_map/reshape | solution.py:65
  221.8 281.9 %all-reduce.7.cloned.1.call-done = f32[18432,128]{1,0:T(8,128)} async-done(((f32[18432,128]{1,0:T(8,128)}), f32[18432,128]{1,0:T(8,128)}) %all-reduce.7.cloned.1.call-update) | async-done | bytes 9437200
  503.7 1.4 multiply_reduce_fusion.4
  506.4 1.3 multiply_reduce_fusion.8
  510.3 9.2 %all-reduce.3 = (f32[]{:T(128)}, f32[]{:T(128)}) all-reduce(f32[]{:T(128)} %get-tuple-element.30, f32[]{:T(128)S(6)} %add.132), channel_id=1, replica_groups=mesh['dp_0'=4,'dp_1'=8,'neg_0'=4,'neg_1'=2] {'dp_0'}, use_global_device_ids=true, to_apply=%region_6.7 | all-reduce | flops 2 | bytes 16 | tf_op jit(solution)/shard_map/psum | solution.py:56
  519.6 15.1 %all-reduce.1 = (f32[]{:T(128)}, f32[]{:T(128)}) all-reduce(f32[]{:T(128)} %get-tuple-element.17, f32[]{:T(128)} %get-tuple-element.18), channel_id=1, replica_groups=mesh['dp_0'=4,'dp_1'=8,'neg_0'=4,'neg_1'=2] {'dp_1'}, use_global_device_ids=true, to_apply=%region_7.8 | all-reduce | flops 2 | bytes 16 | tf_op jit(solution)/shard_map/psum | solution.py:56
  534.7 8.3 %all-reduce.2 = (f32[]{:T(128)}, f32[]{:T(128)}) all-reduce(f32[]{:T(128)} %get-tuple-element.13, f32[]{:T(128)} %get-tuple-element.14), channel_id=1, replica_groups=mesh['dp_0'=4,'dp_1'=8,'neg_0'=4,'neg_1'=2] {'neg_0'}, use_global_device_ids=true, to_apply=%region_8.9 | all-reduce | flops 2 | bytes 16 | tf_op jit(solution)/shard_map/psum | solution.py:56
  543.0 8.3 %all-reduce.4 = (f32[]{:T(128)}, f32[]{:T(128)}) all-reduce(f32[]{:T(128)} %get-tuple-element.15, f32[]{:T(128)} %get-tuple-element.16), channel_id=1, replica_groups=mesh['dp_0'=4,'dp_1'=8,'neg_0'=4,'neg_1'=2] {'neg_1'}, use_global_device_ids=true, to_apply=%region_9.10 | all-reduce | flops 2 | bytes 16 | tf_op jit(solution)/shard_map/psum | solution.py:56
  552.1 0.7 constant_dynamic-update-slice_fusion.8
  552.8 0.7 bitcast_dynamic-update-slice_fusion.2
  553.5 0.7 constant_dynamic-update-slice_fusion.10
  554.2 0.7 bitcast_dynamic-update-slice_fusion.1
  554.9 0.7 bitcast_dynamic-update-slice_fusion
  555.6 0.7 constant_dynamic-update-slice_fusion.9
  556.3 13.0 %all-gather = f32[73728]{0:T(1024)S(1)} all-gather(f32[9216]{0:T(1024)S(1)} %constant_dynamic-update-slice_fusion.9), channel_id=2, replica_groups=mesh['dp_0'=4,'dp_1'=8,'neg_0'=4,'neg_1'=2] {'neg_0','neg_1'}, dimensions={0}, use_global_device_ids=true | all-gather | bytes 331776 | tf_op jit(solution)/shard_map/all_gather | solution.py:76
  (80 shorter events, 7.9 us)
Async XLA Ops:
  7.2 4.5 copy-start
  7.2 5.9 %copy-start.20 = (bf16[512,256]{1,0:T(8,128)(2,1)S(1)}, bf16[512,256]{1,0:T(8,128)(2,1)}, u32[]{:S(2)}) copy-start(bf16[512,256]{1,0:T(8,128)(2,1)} %param.25) | copy-start | bytes 786436
  7.2 6.3 %copy-start.19 = (bf16[256,512]{1,0:T(8,128)(2,1)S(1)}, bf16[256,512]{1,0:T(8,128)(2,1)}, u32[]{:S(2)}) copy-start(bf16[256,512]{1,0:T(8,128)(2,1)} %param.13) | copy-start | bytes 786436
  7.2 6.3 %copy-start.14 = (bf16[512,1024]{1,0:T(8,128)(2,1)S(1)}, bf16[512,1024]{1,0:T(8,128)(2,1)}, u32[]{:S(2)}) copy-start(bf16[512,1024]{1,0:T(8,128)(2,1)} %param.20) | copy-start | bytes 3145732
  7.2 6.7 %copy-start.26 = (bf16[1024,512]{1,0:T(8,128)(2,1)S(1)}, bf16[1024,512]{1,0:T(8,128)(2,1)}, u32[]{:S(2)}) copy-start(bf16[1024,512]{1,0:T(8,128)(2,1)} %param.21) | copy-start | bytes 3145732
  9.2 0.7 copy-start.11
  11.7 3.6 copy-start.8
  11.7 3.6 copy-start.21
  13.1 3.4 copy-start.6
  13.9 2.5 copy-start.15
  13.9 36.9 %copy-start.24 = (s32[2048]{0:T(1024)S(1)}, s32[2048]{0:T(1024)}, u32[]{:S(2)}) copy-start(s32[2048]{0:T(1024)} %param.19) | copy-start | bytes 24580
  14.0 61.9 %copy-start.22 = (s32[2048]{0:T(1024)S(1)}, s32[2048]{0:T(1024)}, u32[]{:S(2)}) copy-start(s32[2048]{0:T(1024)} %param.18) | copy-start | bytes 24580
  14.0 61.9 %copy-start.23 = (s32[2048]{0:T(1024)S(1)}, s32[2048]{0:T(1024)}, u32[]{:S(2)}) copy-start(s32[2048]{0:T(1024)} %param.16) | copy-start | bytes 24580
  15.2 1.2 copy-start.13
  15.6 0.7 copy-start.2
  15.7 69.4 %copy-start.3 = (bf16[320,256]{1,0:T(8,128)(2,1)}, bf16[320,256]{1,0:T(8,128)(2,1)S(1)}, u32[]{:S(2)}) copy-start(bf16[320,256]{1,0:T(8,128)(2,1)S(1)} %multiply_convert_fusion.4) | copy-start | bytes 491524
  16.5 68.6 %copy-start.10 = (bf16[256,256]{1,0:T(8,128)(2,1)}, bf16[256,256]{1,0:T(8,128)(2,1)S(1)}, u32[]{:S(2)}) copy-start(bf16[256,256]{1,0:T(8,128)(2,1)S(1)} %get-tuple-element.22) | copy-start | bytes 393220
  17.6 21.7 %all-to-all-start = ((bf16[8,256,256]{2,1,0:T(8,128)(2,1)}), bf16[8,256,256]{2,1,0:T(8,128)(2,1)S(1)}, u32[]{:S(2)}, u32[]{:S(2)}) async-start(bf16[8,256,256]{2,1,0:T(8,128)(2,1)} %broadcast_in_dim.10), calls=%async_computation | async-start | bytes 2097152 | tf_op jit(solution)/shard_map/all_to_all | solution.py:25
  40.3 35.5 %all-to-all-start.1 = ((bf16[32,64,256]{2,1,0:T(8,128)(2,1)}), bf16[32,64,256]{2,1,0:T(8,128)(2,1)}, u32[]{:S(2)}, u32[]{:S(2)}) async-start(bf16[32,64,256]{2,1,0:T(8,128)(2,1)} %broadcast_in_dim.11), calls=%async_computation.1 | async-start | bytes 2097152 | tf_op jit(solution)/shard_map/all_to_all | solution.py:25
  50.8 109.3 %reduce-scatter.3.cloned.1.call-start = ((), (), s32[]{:S(2)}) async-start(), calls=%async_computation.6 | async-start | bytes 2621440 | tf_op jit(solution)/shard_map/reduce_scatter | solution.py:50
  75.9 9.2 %copy-start.25 = (s32[256]{0:T(256)S(1)}, s32[256]{0:T(256)}, u32[]{:S(2)}) copy-start(s32[256]{0:T(256)} %param.17) | copy-start | bytes 3076
  105.7 3.2 copy-start.1
  120.1 30.5 %all-to-all-start.3 = ((f32[8,256,256]{2,1,0:T(8,128)}), f32[8,256,256]{2,1,0:T(8,128)S(1)}, u32[]{:S(2)}, u32[]{:S(2)}) async-start(f32[8,256,256]{2,1,0:T(8,128)} %fusion.25), calls=%async_computation.3 | async-start | bytes 4194304 | tf_op jit(solution)/shard_map/all_to_all | solution.py:44
  124.3 63.7 %reduce-scatter.5.cloned.1.call-start = ((), (), s32[]{:S(2)}) async-start(), calls=%async_computation.7 | async-start | bytes 589824 | tf_op jit(solution)/shard_map/reduce_scatter | solution.py:50
  154.7 0.6 copy-start.18
  160.1 343.6 %all-reduce.7.cloned.1.call-start = ((), (), s32[]{:S(2)}) async-start(), calls=%async_computation.8 | async-start | bytes 18874368
  174.5 4.8 copy-start.5
  175.9 17.4 %copy-start.9 = (f32[320,1024]{1,0:T(8,128)S(1)}, f32[320,1024]{1,0:T(8,128)}, u32[]{:S(2)}) copy-start(f32[320,1024]{1,0:T(8,128)} %copy-done.8) | copy-start | bytes 3932164
  175.9 17.4 %copy-start.12 = (bf16[320,512]{1,0:T(8,128)(2,1)S(1)}, bf16[320,512]{1,0:T(8,128)(2,1)}, u32[]{:S(2)}) copy-start(bf16[320,512]{1,0:T(8,128)(2,1)} %copy-done.11) | copy-start | bytes 983044
  191.1 0.7 copy-start.16
  193.3 4.7 copy-start.7
  193.4 4.7 copy-start.17
  206.3 4.7 copy-start.4
Sparse Core Ops, SparseCore 0:
  112.9 26.8 reduce-scatter.2
  160.2 27.7 reduce-scatter.4
  221.9 281.7 all-reduce.6
where the time goes:
time: 583 us; the launch traced here: 582 us
  waiting for transfers between devices  355 us (61%)
  blocking collectives  65.9 us (11%)
  local copies, waits for them, and re-layouts  51.1 us (9%)
  matrix products  43.1 us (7%)
  other arithmetic  23.8 us (4%)
  starting transfers between devices  21.7 us (4%)
  between operations  20.6 us (4%)
    unnamed x4, waiting for transfers between devices  282 us
    psum x4, blocking collectives, by_axis(): array = lax.psum(array, axis)  41 us
    all_to_all x2, waiting for transfers between devices, from_everyone(): return lax.all_to_all(copies, axis, split_axis=0, concat_axis=0, tiled=True)  40 us
    all_to_all x1, waiting for transfers between devices, sent_and_summed(): lax.all_to_all(cut_along(array, dim, length), axis, 0, 0, tiled=True)  25.5 us
    dot_general x7, matrix products, contract_rows(): lax.dot_general(left, right, (((0,), (0,)), ((), ())), preferred_element_...  17.5 us
    unnamed x60, local copies, waits for them, and re-layouts  17.4 us
    all_to_all x2, starting transfers between devices, from_everyone(): return lax.all_to_all(copies, axis, split_axis=0, concat_axis=0, tiled=True)  17.1 us
    another operation x6, local copies, waits for them, and re-layouts, cut_along(): array.reshape(*shape[:dim], length, shape[dim] // length, *shape[dim + 1:])  14.2 us
  transfers between devices with their start and end apart: 6, of which 5 were waited for; matrix products, arithmetic and copies ran while one was open for 6% of the time, Pallas kernels for 0%

commit v1 on v0

--- a/solution.py
+++ b/solution.py
@@ -1,6 +1,8 @@
 import jax
 import jax.numpy as jnp
 from jax import lax
+from jax.experimental import pallas as pl
+from jax.experimental.pallas import tpu as pltpu
 from jax.sharding import Mesh
 from jax.sharding import PartitionSpec as P
 
@@ -8,7 +10,10 @@
 DP = ("dp_0", "dp_1")
 DP_NEG = ("dp_0", "dp_1", "neg_0", "neg_1")
 NEG_DP = ("neg_0", "neg_1", "dp_0", "dp_1")
-
+AX_Y, AX_Z, AX_X, AX_C = "dp_0", "dp_1", "neg_0", "neg_1"
+MESH = pl.DeviceIdType.MESH
+F32 = jnp.float32
+BF16 = jnp.bfloat16
 
 inv_temp = 20.0
 clip_norm = 256.0
@@ -49,36 +54,6 @@
     for axis in axes:
         so_far = lax.psum_scatter(so_far, axis, scatter_dimension=0, tiled=True)
     return so_far
-
-
-def by_axis(array, axes):
-    for axis in axes:
-        array = lax.psum(array, axis)
-    return array
-
-
-def one_scatter(arrays, axis, dims):
-    length = lax.axis_size(axis)
-    tiles = [cut_along(a, dim, length) for a, dim in zip(arrays, dims)]
-    lines = jnp.concatenate([b.reshape(length, -1) for b in tiles], axis=1)
-    width = max(16, -(-lines.shape[1] // 1024) * 8)
-    lines = jnp.pad(lines, ((0, 0), (0, width * 128 - lines.shape[1]))).reshape(-1, 128)
-    vector, at, finished = (lax.psum_scatter(lines, axis, tiled=True).reshape(-1), 0, [])
-    for b in tiles:
-        part = b[0]
-        finished.append(vector[at : at + part.size].reshape(part.shape))
-        at += part.size
-    return tuple(finished)
-
-
-def gather_together(arrays, axis, dims):
-    vector = jnp.concatenate([a.reshape(-1) for a in arrays])
-    lines, at, finished = (lax.all_gather(vector, axis), 0, [])
-    for a, dim in zip(arrays, dims):
-        tiles = lines[:, at : at + a.size].reshape(-1, *a.shape)
-        finished.append(laid_out(tiles, dim))
-        at += a.size
-    return tuple(finished)
 
 
 def silu_slope(pre):
@@ -121,6 +96,352 @@
     first_slope = (contract_cols(second_slope, second) * silu_slope(first_pre)).astype(jnp.bfloat16)
     first_grad = contract_rows(features, first_slope)
     return (first_grad, second_grad, third_grad)
+
+
+class Links:
+    def __init__(self, send_sems, recv_sems, size):
+        self.send_sems, self.recv_sems, self.size = send_sems, recv_sems, size
+        self.used = 0
+        self.started = []
+
+    def copy(self, src, dst, device):
+        at = self.used
+        self.used += 1
+        assert at < self.size
+        made = pltpu.make_async_remote_copy(
+            src_ref=src,
+            dst_ref=dst,
+            send_sem=self.send_sems.at[at],
+            recv_sem=self.recv_sems.at[at],
+            device_id=device,
+            device_id_type=MESH,
+        )
+        made.start()
+        self.started.append(made)
+        return made
+
+    def finish(self):
+        for made in self.started:
+            made.wait_send()
+
+
+def add_rows(out, terms, rows, step):
+    def body(i, carry):
+        at = pl.ds(pl.multiple_of(i * step, step), step)
+        total = terms[0][at].astype(F32)
+        for term in terms[1:]:
+            total = total + term[at].astype(F32)
+        out[at] = total.astype(out.dtype)
+        return carry
+
+    if rows == step:
+        body(0, 0)
+    else:
+        lax.fori_loop(0, rows // step, body, 0)
+
+
+class Ring4:
+    def __init__(self, links, axis, cut, rows, land, step):
+        self.links, self.axis, self.cut, self.rows, self.step = links, axis, cut, rows, step
+        self.early_up, self.early_down, self.from_down, self.from_up = land
+        me = lax.axis_index(axis)
+        self.me = me
+        self.up, self.down, self.far = lax.rem(me + 1, 4), lax.rem(me + 3, 4), lax.rem(me + 2, 4)
+
+    def start(self):
+        half = self.rows // 2
+        low, high = pl.ds(0, half), pl.ds(half, half)
+        up, down = {self.axis: self.up}, {self.axis: self.down}
+        far = self.cut(self.far)
+        self.a = self.links.copy(far.at[low], self.early_up, up)
+        self.b = self.links.copy(far.at[high], self.early_down, down)
+        self.c = self.links.copy(self.cut(self.up).at[high], self.from_down.at[high], up)
+        self.d = self.links.copy(self.cut(self.down).at[low], self.from_up.at[low], down)
+
+    def relay(self):
+        half = self.rows // 2
+        low, high = pl.ds(0, half), pl.ds(half, half)
+        up, down = {self.axis: self.up}, {self.axis: self.down}
+        self.a.wait_recv()
+        mine = self.cut(self.up).at[low]
+        add_rows(self.early_up, (mine, self.early_up), half, self.step)
+        self.e = self.links.copy(self.early_up, self.from_down.at[low], up)
+        self.b.wait_recv()
+        mine = self.cut(self.down).at[high]
+        add_rows(self.early_down, (mine, self.early_down), half, self.step)
+        self.f = self.links.copy(self.early_down, self.from_up.at[high], down)
+
+    def end(self, out):
+        for made in (self.c, self.d, self.e, self.f):
+            made.wait_recv()
+        add_rows(out, (self.cut(self.me), self.from_down, self.from_up), self.rows, self.step)
+
+
+class Direct:
+    def __init__(self, links, axis, size, slots):
+        self.links, self.axis, self.size, self.slots = links, axis, size, slots
+        self.me = lax.axis_index(axis)
+
+    def start(self, cut):
+        self.made = []
+        for k in range(1, self.size):
+            to = lax.rem(self.me + k, self.size)
+            self.made.append(self.links.copy(cut(to), self.slots.at[self.me], {self.axis: to}))
+
+    def wait(self):
+        for made in self.made:
+            made.wait_recv()
+
+
+def greet_neighbours():
+    y, z, x, c = (lax.axis_index(a) for a in (AX_Y, AX_Z, AX_X, AX_C))
+    barrier = pltpu.get_barrier_semaphore()
+    peers = [{AX_Y: lax.rem(y + k, 4)} for k in range(1, 4)]
+    peers += [{AX_Z: lax.rem(z + k, 8)} for k in range(1, 8)]
+    for k in range(1, 8):
+        other = lax.rem(x * 2 + c + k, 8)
+        peers.append({AX_X: other // 2, AX_C: lax.rem(other, 2)})
+    for peer in peers:
+        pl.semaphore_signal(barrier, inc=1, device_id=peer, device_id_type=MESH)
+    return barrier, len(peers)
+
+
+def multiple(index, size):
+    return pl.multiple_of(index * size, size)
+
+
+def reduce_gradients(links, g_first, g_second, g_third, loss_tile, outs, bufs):
+    (o_first, o_second, o_third, o_loss) = outs
+    y, z, x, c = (lax.axis_index(a) for a in (AX_Y, AX_Z, AX_X, AX_C))
+    other = {AX_C: 1 - c}
+    mate = 1 - c
+
+    a_first, a_second, a_third = bufs["a_first"], bufs["a_second"], bufs["a_third"]
+    pair = [
+        links.copy(g_first.at[mate], a_first, other),
+        links.copy(g_second.at[mate], a_second, other),
+        links.copy(g_third.at[mate], a_third, other),
+    ]
+    first_x = Ring4(
+        links, AX_X, lambda j: a_first.at[:, pl.ds(multiple(j, 256), 256)], 512, bufs["fx"], 64
+    )
+    second_y = Ring4(
+        links, AX_Y, lambda j: a_second.at[pl.ds(multiple(j, 256), 256)], 256, bufs["sy"], 32
+    )
+    pair[0].wait_recv()
+    add_rows(a_first, (a_first, g_first.at[c]), 512, 16)
+    first_x.start()
+    pair[1].wait_recv()
+    add_rows(a_second, (a_second, g_second.at[c]), 1024, 32)
+    second_y.start()
+    pair[2].wait_recv()
+    for i in range(4):
+        add_rows(a_third.at[i], (a_third.at[i], g_third.at[c, i]), 8, 1)
+    third_z = Direct(links, AX_Z, 8, bufs["tz"])
+    third_z.start(lambda j: a_third.at[:, j])
+
+    first_x.relay()
+    second_y.relay()
+
+    third_z.wait()
+    tz, t_sum = bufs["tz"], bufs["t_sum"]
+    for i in range(4):
+        tz[z, i] = a_third[i, z]
+    for i in range(4):
+        total = tz[0, i].astype(F32)
+        for j in range(1, 8):
+            total = total + tz[j, i].astype(F32)
+        t_sum[i] = total.astype(BF16)
+    third_y = Direct(links, AX_Y, 4, bufs["ty"])
+    third_y.start(lambda j: t_sum.at[j])
+
+    fx_sum, sy_sum = bufs["fx_sum"], bufs["sy_sum"]
+    first_x.end(fx_sum)
+    first_y = Ring4(
+        links, AX_Y, lambda j: fx_sum.at[pl.ds(multiple(j, 128), 128)], 128, bufs["fy"], 64
+    )
+    first_y.start()
+    second_y.end(sy_sum)
+    second_x = Ring4(
+        links, AX_X, lambda j: sy_sum.at[:, pl.ds(multiple(j, 128), 128)], 256, bufs["sx"], 128
+    )
+    second_x.start()
+
+    third_y.wait()
+    ty, ty_sum = bufs["ty"], bufs["ty_sum"]
+    ty[y] = t_sum[y]
+    total = ty[0].astype(F32)
+    for j in range(1, 4):
+        total = total + ty[j].astype(F32)
+    ty_sum[...] = total.astype(BF16)
+    third_x = Direct(links, AX_X, 4, bufs["tx"])
+    third_x.start(lambda j: ty_sum)
+
+    first_y.relay()
+    second_x.relay()
+    fy_sum, sx_sum = bufs["fy_sum"], bufs["sx_sum"]
+    first_y.end(fy_sum)
+    first_z = Direct(links, AX_Z, 8, bufs["fz"])
+    first_z.start(lambda j: fy_sum.at[pl.ds(multiple(j, 16), 16)])
+    second_x.end(sx_sum)
+    second_z = Direct(links, AX_Z, 8, bufs["sz"])
+    second_z.start(lambda j: sx_sum.at[pl.ds(multiple(j, 32), 32)])
+
+    third_x.wait()
+    tx = bufs["tx"]
+    tx[x] = ty_sum[...]
+    t_final = tx[0].astype(F32)
+    for j in range(1, 4):
+        t_final = t_final + tx[j].astype(F32)
+
+    first_z.wait()
+    f_final = fy_sum[pl.ds(multiple(z, 16), 16), :].astype(F32)
+    fz, sz = bufs["fz"], bufs["sz"]
+    fz[z] = fy_sum[pl.ds(multiple(z, 16), 16), :]
+    f_final = fz[0].astype(F32)
+    for j in range(1, 8):
+        f_final = f_final + fz[j].astype(F32)
+    second_z.wait()
+    sz[z] = sx_sum[pl.ds(multiple(z, 32), 32), :]
+    s_final = sz[0].astype(F32)
+    for j in range(1, 8):
+        s_final = s_final + sz[j].astype(F32)
+
+    squares = jnp.sum((f_final * f_final).reshape(2, 8, 2, 128), axis=(0, 2))
+    squares += jnp.sum((s_final * s_final).reshape(4, 8, 128), axis=0)
+    squares += jnp.sum((t_final * t_final).reshape(2, 8, 2, 128), axis=(0, 2)) * 0.25
+    f_own, s_own, t_own = bufs["f_own"], bufs["s_own"], bufs["t_own"]
+    c_in, c_out, y_in, y_out, z_in, z_out = (
+        bufs[k] for k in ("c_in", "c_out", "y_in", "y_out", "z_in", "z_out")
+    )
+    c_out[0] = squares
+    c_out[1] = loss_tile[...]
+    f_own[...] = f_final
+    s_own[...] = s_final
+    t_own[...] = t_final
+    me = x * 2 + c
+    others = []
+    for k in range(1, 8):
+        to = lax.rem(me + k, 8)
+        others.append({AX_X: to // 2, AX_C: lax.rem(to, 2)})
+    scalars = [links.copy(c_out, c_in.at[me], peer) for peer in others]
+    ag_first, ag_second, ag_third = bufs["ag_first"], bufs["ag_second"], bufs["ag_third"]
+    f_cols = pl.ds(multiple(x, 256), 256)
+    s_cols = pl.ds(multiple(x, 128), 128)
+    pieces = [links.copy(t_own, ag_third.at[c], other)]
+    for peer in others:
+        pieces.append(links.copy(f_own, ag_first.at[c, :, f_cols], peer))
+        pieces.append(links.copy(s_own, ag_second.at[c, :, s_cols], peer))
+    c_in[me] = c_out[...]
+    ag_first[c, :, f_cols] = f_final
+    ag_second[c, :, s_cols] = s_final
+    ag_third[c] = t_final
+    for made in scalars:
+        made.wait_recv()
+    total = c_in[0]
+    for j in range(1, 8):
+        total = total + c_in[j]
+    y_out[...] = total
+    y_in[y] = total
+    along_y = Direct(links, AX_Y, 4, y_in)
+    along_y.start(lambda j: y_out)
+    along_y.wait()
+    total = y_in[0]
+    for j in range(1, 4):
+        total = total + y_in[j]
+    z_out[...] = total
+    z_in[z] = total
+    along_z = Direct(links, AX_Z, 8, z_in)
+    along_z.start(lambda j: z_out)
+    along_z.wait()
+    total = z_in[0]
+    for j in range(1, 8):
+        total = total + z_in[j]
+    norm = jnp.sqrt(jnp.sum(total[0], keepdims=True))
+    factor = clip_norm / jnp.maximum(norm, clip_norm)
+    o_loss[...] = jnp.broadcast_to(jnp.sum(total[1], keepdims=True), (8, 128))
+    for made in pieces:
+        made.wait_recv()
+    for t in range(2):
+        o_first[t] = ag_first[t] * factor
+        o_second[t] = ag_second[t] * factor
+        o_third[t] = ag_third[t] * factor
+
+
+LINKS = 120
+
+
+def ring_land(rows, cols):
+    half = pltpu.VMEM((rows // 2, cols), BF16)
+    whole = pltpu.VMEM((rows, cols), BF16)
+    return (half, half, whole, whole)
+
+
+GRAD_BUFS = {
+    "a_first": pltpu.VMEM((512, 1024), BF16),
+    "a_second": pltpu.VMEM((1024, 512), BF16),
+    "a_third": pltpu.VMEM((4, 8, 16, 256), BF16),
+    "fx": ring_land(512, 256),
+    "sy": ring_land(256, 512),
+    "tz": pltpu.VMEM((8, 4, 16, 256), BF16),
+    "t_sum": pltpu.VMEM((4, 16, 256), BF16),
+    "ty": pltpu.VMEM((4, 16, 256), BF16),
+    "ty_sum": pltpu.VMEM((16, 256), BF16),
+    "tx": pltpu.VMEM((4, 16, 256), BF16),
+    "fx_sum": pltpu.VMEM((512, 256), BF16),
+    "sy_sum": pltpu.VMEM((256, 512), BF16),
+    "fy": ring_land(128, 256),
+    "sx": ring_land(256, 128),
+    "fy_sum": pltpu.VMEM((128, 256), BF16),
+    "sx_sum": pltpu.VMEM((256, 128), BF16),
+    "fz": pltpu.VMEM((8, 16, 256), BF16),
+    "sz": pltpu.VMEM((8, 32, 128), BF16),
+    "f_own": pltpu.VMEM((16, 256), F32),
+    "s_own": pltpu.VMEM((32, 128), F32),
+    "t_own": pltpu.VMEM((16, 256), F32),
+    "c_in": pltpu.VMEM((8, 2, 8, 128), F32),
+    "c_out": pltpu.VMEM((2, 8, 128), F32),
+    "y_in": pltpu.VMEM((4, 2, 8, 128), F32),
+    "y_out": pltpu.VMEM((2, 8, 128), F32),
+    "z_in": pltpu.VMEM((8, 2, 8, 128), F32),
+    "z_out": pltpu.VMEM((2, 8, 128), F32),
+    "ag_first": pltpu.VMEM((2, 16, 1024), F32),
+    "ag_second": pltpu.VMEM((2, 32, 512), F32),
+    "ag_third": pltpu.VMEM((2, 16, 256), F32),
+}
+
+
+def gradient_kernel(g_first, g_second, g_third, loss, o_first, o_second, o_third, o_loss, bufs, send, recv):
+    barrier, peers = greet_neighbours()
+    pl.semaphore_wait(barrier, peers)
+    links = Links(send, recv, LINKS)
+    outs = (o_first, o_second, o_third, o_loss)
+    reduce_gradients(links, g_first, g_second, g_third, loss, outs, bufs)
+    links.finish()
+
+
+def reduced_gradients(g_first, g_second, g_third, loss):
+    vmem = pl.BlockSpec(memory_space=pltpu.VMEM)
+    return pl.pallas_call(
+        gradient_kernel,
+        out_shape=(
+            jax.ShapeDtypeStruct((2, 16, 1024), F32),
+            jax.ShapeDtypeStruct((2, 32, 512), F32),
+            jax.ShapeDtypeStruct((2, 16, 256), F32),
+            jax.ShapeDtypeStruct((8, 128), F32),
+        ),
+        in_specs=[vmem] * 4,
+        out_specs=(vmem,) * 4,
+        scratch_shapes=[
+            GRAD_BUFS,
+            pltpu.SemaphoreType.DMA((LINKS,)),
+            pltpu.SemaphoreType.DMA((LINKS,)),
+        ],
+        compiler_params=pltpu.CompilerParams(
+            collective_id=0, has_side_effects=True, vmem_limit_bytes=60 * 1024 * 1024
+        ),
+        name="reduce_gradients",
+    )(g_first, g_second, g_third, loss)
 
 
 def per_device(
@@ -177,28 +498,15 @@
     item_grad = jnp.concatenate([positive_grad, negative_sum * inv_temp], axis=0)
     query_grads = tower_backward(query_features, query_second, query_third, query_saved, query_grad)
     item_grads = tower_backward(item_features, item_second, item_third, item_saved, item_grad)
-    gradients = query_grads + item_grads
-    loss_sum = by_axis(loss_part, DP_NEG)
-    mean_loss = loss_sum / (own_rows * lax.axis_size(DP) * lax.axis_size(NEG))
-    vectors = tuple((gradient.reshape(-1) for gradient in gradients))
-    pieces = one_scatter(
-        (vectors[0], vectors[1], vectors[2], vectors[3], vectors[4], vectors[5]),
-        DP_NEG,
-        (0, 0, 0, 0, 0, 0),
-    )
-    squares = jnp.zeros((), jnp.float32)
-    for piece in pieces:
-        squares = squares + jnp.sum(piece * piece)
-    grad_norm = jnp.sqrt(by_axis(squares, DP_NEG))
-    clip_factor = clip_norm / jnp.maximum(grad_norm, clip_norm)
-    scaled = tuple((piece * clip_factor for piece in pieces))
-    gathered = gather_together(
-        (scaled[0], scaled[1], scaled[2], scaled[3], scaled[4], scaled[5]), NEG, (0, 0, 0, 0, 0, 0)
-    )
-    clipped = tuple(
-        (vector.reshape(-1, gradient.shape[1]) for vector, gradient in zip(gathered, gradients))
-    )
-    return (mean_loss, clipped[0], clipped[1], clipped[2], clipped[3], clipped[4], clipped[5])
+    stacked = [
+        jnp.stack([a.astype(BF16), b.astype(BF16)]) for a, b in zip(query_grads, item_grads)
+    ]
+    loss_tile = jnp.broadcast_to(loss_part * (1.0 / 1024.0), (8, 128))
+    first, second, third, loss = reduced_gradients(
+        stacked[0], stacked[1], stacked[2].reshape(2, 4, 8, 16, 256), loss_tile
+    )
+    mean_loss = loss[0, 0] / (own_rows * lax.axis_size(DP) * lax.axis_size(NEG))
+    return (mean_loss, first[0], second[0], third[0], first[1], second[1], third[1])
 
 
 def solution(mesh):

time: 583 us -> 263 us (0.45)
  waiting for transfers between devices: 355 us -> 85.7 us
  blocking collectives: 65.9 us -> 11.8 us
  Pallas kernels: 0 us -> 52.8 us
  local copies, waits for them, and re-layouts: 51.1 us -> 15.2 us
    unnamed x4 -> x2, waiting for transfers between devices: 282 us -> 0.03 us
    pallas_call x0 -> x1, Pallas kernels: none -> 52.8 us  [reduced_gradients(): pl.pallas_call(gradient_kernel, out_shape=(jax.ShapeDtypeStruct((2, 16, 1...]
    psum x4 -> x0, blocking collectives: 41 us -> none  [by_axis(): array = lax.psum(array, axis)]
    another operation x12 -> x0, local copies, waits for them, and re-layouts: 17.9 us -> none  [the longest x6 14.2 us: cut_along(): array.reshape(*shape[:dim], length, shape[dim] // length, *shape[dim + 1:])]
    all_gather x1 -> x0, blocking collectives: 13 us -> none  [gather_together(): lines, at, finished = (lax.all_gather(vector, axis), 0, [])]
    reduce_scatter x2, waiting for transfers between devices: 7.92 us -> 20.8 us  [own_rows_2(): so_far = lax.psum_scatter(so_far, axis, scatter_dimension=0, tiled=True)]
    unnamed x60 -> x59, local copies, waits for them, and re-layouts: 17.4 us -> 6.79 us
    reshape x1 -> x0, local copies, waits for them, and re-layouts: 9.91 us -> none  [one_scatter(): jnp.pad(lines, ((0, 0), (0, width * 128 - lines.shape[1]))).reshape(-1, 128)]
  transfers between devices with their start and end apart: 6 -> 5, of which waited for: 5 -> 4; matrix products, arithmetic and copies ran while one was open for 6% -> 7% of each run, Pallas kernels for 0% -> 0%
where the time goes in v1:
time: 263 us; the launch traced here: 262 us
  waiting for transfers between devices  85.7 us (33%)
  Pallas kernels  52.8 us (20%)
  matrix products  38.3 us (15%)
  starting transfers between devices  21.4 us (8%)
  other arithmetic  19.8 us (8%)
  between operations  16.8 us (6%)
  local copies, waits for them, and re-layouts  15.2 us (6%)
  blocking collectives  11.8 us (4%)
    pallas_call x1, Pallas kernels, reduced_gradients(): pl.pallas_call(gradient_kernel, out_shape=(jax.ShapeDtypeStruct((2, 16, 1...  52.8 us
    all_to_all x2, waiting for transfers between devices, from_everyone(): return lax.all_to_all(copies, axis, split_axis=0, concat_axis=0, tiled=True)  40 us
    all_to_all x1, waiting for transfers between devices, sent_and_summed(): lax.all_to_all(cut_along(array, dim, length), axis, 0, 0, tiled=True)  24.9 us
    reduce_scatter x2, waiting for transfers between devices, own_rows_2(): so_far = lax.psum_scatter(so_far, axis, scatter_dimension=0, tiled=True)  20.8 us
    all_to_all x2, starting transfers between devices, from_everyone(): return lax.all_to_all(copies, axis, split_axis=0, concat_axis=0, tiled=True)  17.1 us
    dot_general x7, matrix products, contract_rows(): lax.dot_general(left, right, (((0,), (0,)), ((), ())), preferred_element_...  13.4 us
    all_to_all x1, blocking collectives, from_everyone(): return lax.all_to_all(copies, axis, split_axis=0, concat_axis=0, tiled=True)  11.8 us
    dot_general x3, matrix products, contract_cols(): lax.dot_general(left, right, (((1,), (1,)), ((), ())), preferred_element_...  11 us
  transfers between devices with their start and end apart: 5, of which 4 were waited for; matrix products, arithmetic and copies ran while one was open for 7% of the time, Pallas kernels for 0%

profile of v1, /device:TPU:1, one launch (start us, length us, event | category | flops | bytes accessed | tf_op | source)
XLA Modules:
  0.0 262.0 jit_solution(4124238459371866718)
XLA Ops:
  7.2 0.0 copy-start
  7.2 0.0 copy-start.26
  7.2 1.1 constant_dynamic-update-slice_fusion.1
  8.3 1.7 fusion.21
  10.1 0.0 copy-start.17
  10.1 0.0 copy-start.20
  10.1 0.0 copy-start.25
  10.1 1.3 multiply_convert_fusion.3
  11.4 0.3 multiply_reduce_fusion.3
  11.7 0.3 copy-done.25
  12.0 1.6 multiply_convert_fusion
  13.6 1.4 multiply_convert_fusion.2
  15.0 0.3 multiply_reduce_fusion.1
  15.3 0.1 multiply_convert_fusion.4
  15.5 0.2 fusion.16
  15.7 0.0 copy-done.12
  15.7 0.6 copy-done.4
  16.4 1.1 broadcast_in_dim.12
  17.4 6.7 %all-to-all-start = ((bf16[8,256,256]{2,1,0:T(8,128)(2,1)}), bf16[8,256,256]{2,1,0:T(8,128)(2,1)S(1)}, u32[]{:S(2)}, u32[]{:S(2)}) async-start(bf16[8,256,256]{2,1,0:T(8,128)(2,1)} %broadcast_in_dim.12), calls=%async_computation | async-start | bytes 2097152 | tf_op jit(solution)/shard_map/all_to_all | solution.py:30
  24.1 15.0 %all-to-all-done = bf16[8,256,256]{2,1,0:T(8,128)(2,1)S(1)} async-done(((bf16[8,256,256]{2,1,0:T(8,128)(2,1)}), bf16[8,256,256]{2,1,0:T(8,128)(2,1)S(1)}, u32[]{:S(2)}, u32[]{:S(2)}) %all-to-all-start) | async-done | bytes 1048608 | tf_op jit(solution)/shard_map/all_to_all | solution.py:30
  39.1 1.1 broadcast_in_dim.13
  40.2 10.4 %all-to-all-start.1 = ((bf16[32,64,256]{2,1,0:T(8,128)(2,1)}), bf16[32,64,256]{2,1,0:T(8,128)(2,1)}, u32[]{:S(2)}, u32[]{:S(2)}) async-start(bf16[32,64,256]{2,1,0:T(8,128)(2,1)} %broadcast_in_dim.13), calls=%async_computation.1 | async-start | bytes 2097152 | tf_op jit(solution)/shard_map/all_to_all | solution.py:30
  50.6 0.0 reduce-scatter.3.cloned.1.call-start
  50.7 25.0 %all-to-all-done.1 = bf16[32,64,256]{2,1,0:T(8,128)(2,1)} async-done(((bf16[32,64,256]{2,1,0:T(8,128)(2,1)}), bf16[32,64,256]{2,1,0:T(8,128)(2,1)}, u32[]{:S(2)}, u32[]{:S(2)}) %all-to-all-start.1) | async-done | bytes 1048608 | tf_op jit(solution)/shard_map/all_to_all | solution.py:30
  75.7 9.2 %fusion = (f32[2048]{0:T(1024)S(1)}, f32[2048,2048]{1,0:T(8,128)}) fusion(f32[2048]{0:T(1024)S(1)} %convert_log_fusion, s32[2048]{0:T(1024)S(1)} %copy-done.21, s32[2048]{0:T(1024)S(1)} %copy-done.22, bf16[2048,256]{1,0:T(8,128)(2,1)S(1)} %bitcast.65, bf16[2048,256]{1,0:T(8,128)(2,1)} %bitcast.1), kind=kOutput, calls=%fused_computation.2 | convolution fusion | flops 2168453120 | bytes 18907136 | tf_op jit(solution)/shard_map/dot_general | solution.py:71
  84.9 0.2 add_dynamic-update-slice_fusion
  85.1 11.8 %all_to_all.21 = f32[8,1,2048]{2,1,0:T(1,128)S(1)} all-to-all(f32[8,1,2048]{2,1,0:T(1,128)S(1)} %broadcast_in_dim.15), channel_id=1, replica_groups=mesh['dp_0'=4,'dp_1'=8,'neg_0'=4,'neg_1'=2] {'neg_0','neg_1'}, dimensions={0} | all-to-all | bytes 131072 | tf_op jit(solution)/shard_map/all_to_all | solution.py:30
  97.0 0.1 reduce_sum.85
  97.0 8.4 %divide_convert_fusion = bf16[2048,2048]{1,0:T(8,128)(2,1)S(1)} fusion(f32[2048,2048]{1,0:T(8,128)} %get-tuple-element.43, f32[2048]{0:T(1024)S(1)} %reduce_sum.85, f32[2048]{0:T(1024)S(1)} %convert_log_fusion, s32[2048]{0:T(1024)S(1)} %copy-done.21, s32[2048]{0:T(1024)S(1)} %copy-done.22), kind=kLoop, calls=%fused_computation | loop fusion | flops 25165824 | bytes 25198592 | tf_op jit(solution)/shard_map/convert_element_type | solution.py:486
  105.5 3.2 %copy-done.1 = bf16[2048,2048]{1,0:T(8,128)(2,1)} copy-done((bf16[2048,2048]{1,0:T(8,128)(2,1)}, bf16[2048,2048]{1,0:T(8,128)(2,1)S(1)}, u32[]{:S(2)}) %copy-start.1) | copy-done | bytes 8388632
  108.7 3.9 %fusion.23 = f32[2048,256]{1,0:T(8,128)} fusion(bf16[2048,2048]{1,0:T(8,128)(2,1)S(1)} %divide_convert_fusion, bf16[2048,256]{1,0:T(8,128)(2,1)S(1)} %bitcast.66), kind=kOutput, calls=%fused_computation.77 | convolution fusion | flops 2147483648 | bytes 11534336 | tf_op jit(solution)/shard_map/dot_general | solution.py:65
  112.6 0.0 reduce-scatter.3.cloned.1.call-update
  112.6 7.3 %fusion.22 = f32[8,256,256]{2,1,0:T(8,128)} fusion(bf16[8,256,2048]{2,1,0:T(8,128)(2,1)} %bitcast.64, bf16[2048,256,1]{1,0,2:T(8,128)(2,1)} %bitcast.3), kind=kOutput, calls=%fused_computation.76 | convolution fusion | flops 2147483648 | bytes 11534336 | tf_op jit(solution)/shard_map/dot_general | solution.py:490
  119.9 4.3 %all-to-all-start.3 = ((f32[8,256,256]{2,1,0:T(8,128)}), f32[8,256,256]{2,1,0:T(8,128)S(1)}, u32[]{:S(2)}, u32[]{:S(2)}) async-start(f32[8,256,256]{2,1,0:T(8,128)} %fusion.22), calls=%async_computation.3 | async-start | bytes 4194304 | tf_op jit(solution)/shard_map/all_to_all | solution.py:49
  124.2 0.7 subtract_reduce_fusion
  125.6 24.9 %all-to-all-done.3 = f32[8,256,256]{2,1,0:T(8,128)S(1)} async-done(((f32[8,256,256]{2,1,0:T(8,128)}), f32[8,256,256]{2,1,0:T(8,128)S(1)}, u32[]{:S(2)}, u32[]{:S(2)}) %all-to-all-start.3) | async-done | bytes 2097184 | tf_op jit(solution)/shard_map/all_to_all | solution.py:49
  150.5 0.8 reduce_sum.86
  151.3 1.3 multiply_reduce_fusion.2
  152.6 1.3 subtract_convert_fusion.1
  153.9 0.0 reduce-scatter.3.cloned.1.call-done
  154.0 0.0 reduce-scatter.5.cloned.1.call-update
  154.0 0.3 convolution_convert_fusion.5
  154.3 1.4 fusion.8
  155.7 0.7 copy-done.28
  156.4 1.5 fusion.3
  157.9 3.2 %fusion.1 = bf16[1,512,1024]{2,1,0:T(8,128)(2,1)} fusion(bf16[256,512]{1,0:T(8,128)(2,1)S(1)} %copy-done.14, bf16[256,512]{1,0:T(8,128)(2,1)} %copy-done.28, bf16[1024,512]{1,0:T(8,128)(2,1)} %param.21, f32[256,1024]{1,0:T(8,128)S(1)} %copy-done.6), kind=kOutput, calls=%fused_computation.10 | convolution fusion | flops 539754496 | bytes 3670016 | tf_op jit(solution)/shard_map/dot_general | solution.py:65
  161.1 20.8 %reduce-scatter.5.cloned.1.call-done = f32[64,256]{1,0:T(8,128)} async-done(((f32[512,256]{1,0:T(8,128)}), f32[64,256]{1,0:T(8,128)}) %reduce-scatter.5.cloned.1.call-update) | async-done | bytes 65552 | tf_op jit(solution)/shard_map/reduce_scatter | solution.py:55
  181.9 0.9 broadcast_multiply_fusion
  182.8 0.1 multiply_reduce_fusion
  183.0 0.2 subtract_convert_fusion
  183.2 0.3 convolution_convert_fusion.4
  183.6 0.4 fusion.7
  183.9 0.7 copy-done.11
  184.6 0.7 fusion.4
  185.4 3.5 %fusion.2 = bf16[1,512,1024]{2,1,0:T(8,128)(2,1)} fusion(bf16[320,512]{1,0:T(8,128)(2,1)S(1)} %copy-done.19, bf16[320,512]{1,0:T(8,128)(2,1)S(1)} %fusion.7, bf16[1024,512]{1,0:T(8,128)(2,1)S(1)} %copy-done, f32[320,1024]{1,0:T(8,128)} %get-tuple-element.33), kind=kOutput, calls=%fused_computation.11 | convolution fusion | flops 674562048 | bytes 4063232 | tf_op jit(solution)/shard_map/dot_general | solution.py:65
  188.9 0.8 pad_maximum_fusion.2.g_third
  189.7 3.1 %pad_maximum_fusion.g_first = bf16[2,512,1024]{2,1,0:T(8,128)(2,1)} fusion(bf16[1,512,1024]{2,1,0:T(8,128)(2,1)} %fusion.2, bf16[1,512,1024]{2,1,0:T(8,128)(2,1)} %fusion.1), kind=kLoop, calls=%fused_computation.3 | loop fusion | flops 1048576 | bytes 4194304 | tf_op jit(solution)/shard_map/stack | solution.py:502
  192.9 1.5 pad_maximum_fusion.1.g_second
  194.3 0.6 broadcast_in_dim.30.loss
  194.9 52.8 %reduce_gradients.1 = (f32[2,16,1024]{2,1,0:T(8,128)}, f32[2,32,512]{2,1,0:T(8,128)}, f32[2,16,256]{2,1,0:T(8,128)}, f32[8,128]{1,0:T(8,128)}) custom-call(bf16[2,512,1024]{2,1,0:T(8,128)(2,1)} %pad_maximum_fusion.g_first, bf16[2,1024,512]{2,1,0:T(8,128)(2,1)} %pad_maximum_fusion.1.g_second, bf16[2,4,8,16,256]{4,3,2,1,0:T(8,128)(2,1)} %pad_maximum_fusion.2.g_third, ...), custom_call_target="tpu_custom_call" | custom-call | tf_op jit(solution)/shard_map/reduce_gradients/pallas_call | solution.py:425
  247.8 1.2 slice.29
  249.0 1.3 slice_bitcast_fusion.4
  250.3 1.5 slice_bitcast_fusion.1
  251.8 1.5 slice_bitcast_fusion
  (54 shorter events, 0.2 us)
Async XLA Ops:
  7.2 6.4 %copy-start = (bf16[1024,512]{1,0:T(8,128)(2,1)S(1)}, bf16[1024,512]{1,0:T(8,128)(2,1)}, u32[]{:S(2)}) copy-start(bf16[1024,512]{1,0:T(8,128)(2,1)} %param.24) | copy-start | bytes 3145732
  7.2 2.9 %copy-start.26 = (bf16[1024,512]{1,0:T(8,128)(2,1)S(1)}, bf16[1024,512]{1,0:T(8,128)(2,1)}, u32[]{:S(2)}) copy-start(bf16[1024,512]{1,0:T(8,128)(2,1)} %param.21) | copy-start | bytes 3145732
  10.1 1.3 copy-start.5
  10.1 1.3 copy-start.17
  10.1 1.6 copy-start.20
  10.1 1.9 copy-start.25
  11.4 2.2 copy-start.7
  11.7 3.8 %copy-start.2 = (f32[256,256]{1,0:T(8,128)}, f32[256,256]{1,0:T(8,128)S(1)}, u32[]{:S(2)}) copy-start(f32[256,256]{1,0:T(8,128)S(1)} %get-tuple-element.41) | copy-start | bytes 786436
  12.0 1.6 copy-start.18
  13.6 1.4 copy-start.10
  13.6 1.4 copy-start.15
  15.0 0.7 copy-start.12
  15.5 24.7 %copy-start.3 = (bf16[320,256]{1,0:T(8,128)(2,1)}, bf16[320,256]{1,0:T(8,128)(2,1)S(1)}, u32[]{:S(2)}) copy-start(bf16[320,256]{1,0:T(8,128)(2,1)S(1)} %multiply_convert_fusion.4) | copy-start | bytes 491524
  15.7 0.6 copy-start.4
  17.4 21.7 %all-to-all-start = ((bf16[8,256,256]{2,1,0:T(8,128)(2,1)}), bf16[8,256,256]{2,1,0:T(8,128)(2,1)S(1)}, u32[]{:S(2)}, u32[]{:S(2)}) async-start(bf16[8,256,256]{2,1,0:T(8,128)(2,1)} %broadcast_in_dim.12), calls=%async_computation | async-start | bytes 2097152 | tf_op jit(solution)/shard_map/all_to_all | solution.py:30
  24.1 26.6 %copy-start.23 = (s32[2048]{0:T(1024)S(1)}, s32[2048]{0:T(1024)}, u32[]{:S(2)}) copy-start(s32[2048]{0:T(1024)} %param.19) | copy-start | bytes 24580
  24.1 51.6 %copy-start.21 = (s32[2048]{0:T(1024)S(1)}, s32[2048]{0:T(1024)}, u32[]{:S(2)}) copy-start(s32[2048]{0:T(1024)} %param.18) | copy-start | bytes 24580
  24.1 51.6 %copy-start.22 = (s32[2048]{0:T(1024)S(1)}, s32[2048]{0:T(1024)}, u32[]{:S(2)}) copy-start(s32[2048]{0:T(1024)} %param.16) | copy-start | bytes 24580
  40.2 35.5 %all-to-all-start.1 = ((bf16[32,64,256]{2,1,0:T(8,128)(2,1)}), bf16[32,64,256]{2,1,0:T(8,128)(2,1)}, u32[]{:S(2)}, u32[]{:S(2)}) async-start(bf16[32,64,256]{2,1,0:T(8,128)(2,1)} %broadcast_in_dim.13), calls=%async_computation.1 | async-start | bytes 2097152 | tf_op jit(solution)/shard_map/all_to_all | solution.py:30
  50.6 103.3 %reduce-scatter.3.cloned.1.call-start = ((), (), s32[]{:S(2)}) async-start(), calls=%async_computation.6 | async-start | bytes 2621440 | tf_op jit(solution)/shard_map/reduce_scatter | solution.py:55
  75.7 9.2 %copy-start.24 = (s32[256]{0:T(256)S(1)}, s32[256]{0:T(256)}, u32[]{:S(2)}) copy-start(s32[256]{0:T(256)} %param.17) | copy-start | bytes 3076
  105.5 3.3 %copy-start.1 = (bf16[2048,2048]{1,0:T(8,128)(2,1)}, bf16[2048,2048]{1,0:T(8,128)(2,1)S(1)}, u32[]{:S(2)}) copy-start(bf16[2048,2048]{1,0:T(8,128)(2,1)S(1)} %divide_convert_fusion) | copy-start | bytes 25165828
  119.9 30.5 %all-to-all-start.3 = ((f32[8,256,256]{2,1,0:T(8,128)}), f32[8,256,256]{2,1,0:T(8,128)S(1)}, u32[]{:S(2)}, u32[]{:S(2)}) async-start(f32[8,256,256]{2,1,0:T(8,128)} %fusion.22), calls=%async_computation.3 | async-start | bytes 4194304 | tf_op jit(solution)/shard_map/all_to_all | solution.py:49
  124.2 57.7 %reduce-scatter.5.cloned.1.call-start = ((), (), s32[]{:S(2)}) async-start(), calls=%async_computation.7 | async-start | bytes 589824 | tf_op jit(solution)/shard_map/reduce_scatter | solution.py:55
  151.3 2.7 %copy-start.8 = (bf16[256,512]{1,0:T(8,128)(2,1)S(1)}, bf16[256,512]{1,0:T(8,128)(2,1)}, u32[]{:S(2)}) copy-start(bf16[256,512]{1,0:T(8,128)(2,1)} %copy-done.7) | copy-start | bytes 786436
  153.9 2.5 copy-start.6
  155.7 0.7 copy-start.28
  156.4 1.5 copy-start.14
  157.9 25.3 %copy-start.13 = (bf16[320,512]{1,0:T(8,128)(2,1)S(1)}, bf16[320,512]{1,0:T(8,128)(2,1)}, u32[]{:S(2)}) copy-start(bf16[320,512]{1,0:T(8,128)(2,1)} %copy-done.12) | copy-start | bytes 983044
  161.1 22.4 %copy-start.16 = (bf16[512,256]{1,0:T(8,128)(2,1)S(1)}, bf16[512,256]{1,0:T(8,128)(2,1)}, u32[]{:S(2)}) copy-start(bf16[512,256]{1,0:T(8,128)(2,1)} %param.25) | copy-start | bytes 786436
  181.9 1.6 copy-start.27
  183.5 1.1 copy-start.11
  183.6 1.8 copy-start.19
  189.7 3.2 %copy-start.9 = (bf16[1,1024,512]{2,1,0:T(8,128)(2,1)S(1)}, bf16[1,1024,512]{2,1,0:T(8,128)(2,1)}, u32[]{:S(2)}) copy-start(bf16[1,1024,512]{2,1,0:T(8,128)(2,1)} %fusion.3) | copy-start | bytes 3145732
Sparse Core Ops, SparseCore 0:
  112.8 26.8 reduce-scatter.2
  154.1 27.7 reduce-scatter.4

commit v2 on v1

--- a/solution.py
+++ b/solution.py
@@ -17,85 +17,7 @@
 
 inv_temp = 20.0
 clip_norm = 256.0
-
-
-def laid_out(tiles, dim):
-    tiles = jnp.moveaxis(tiles, 0, dim)
-    shape = tiles.shape
-    return tiles.reshape(*shape[:dim], shape[dim] * shape[dim + 1], *shape[dim + 2 :])
-
-
-def from_everyone(array, axis):
-    copies = jnp.broadcast_to(array, (lax.axis_size(axis), *array.shape))
-    return lax.all_to_all(copies, axis, split_axis=0, concat_axis=0, tiled=True)
-
-
-def collect(array, axis, dim):
-    return laid_out(from_everyone(array, axis), dim)
-
-
-def over_copies(array, axis):
-    return from_everyone(array, axis).sum(axis=0)
-
-
-def cut_along(array, dim, length):
-    shape = array.shape
-    tiles = array.reshape(*shape[:dim], length, shape[dim] // length, *shape[dim + 1 :])
-    return jnp.moveaxis(tiles, dim, 0)
-
-
-def sent_and_summed(array, axis, dim):
-    length = lax.axis_size(axis)
-    tiles = lax.all_to_all(cut_along(array, dim, length), axis, 0, 0, tiled=True)
-    return jnp.sum(tiles, axis=0)
-
-
-def own_rows_2(so_far, axes):
-    for axis in axes:
-        so_far = lax.psum_scatter(so_far, axis, scatter_dimension=0, tiled=True)
-    return so_far
-
-
-def silu_slope(pre):
-    sigma = jax.nn.sigmoid(pre)
-    return sigma * (1.0 + pre * (1.0 - sigma))
-
-
-def contract_rows(left, right):
-    return lax.dot_general(
-        left, right, (((0,), (0,)), ((), ())), preferred_element_type=jnp.float32
-    )
-
-
-def contract_cols(left, right):
-    return lax.dot_general(
-        left, right, (((1,), (1,)), ((), ())), preferred_element_type=jnp.float32
-    )
-
-
-def tower_forward(features, first, second, third):
-    first_pre = jnp.dot(features, first, preferred_element_type=jnp.float32)
-    first_act = jax.nn.silu(first_pre).astype(jnp.bfloat16)
-    second_pre = jnp.dot(first_act, second, preferred_element_type=jnp.float32)
-    second_act = jax.nn.silu(second_pre).astype(jnp.bfloat16)
-    embedding = jnp.dot(second_act, third, preferred_element_type=jnp.float32)
-    inv_norm = lax.rsqrt(jnp.sum(embedding * embedding, axis=1, keepdims=True) + 1.0)
-    unit = (embedding * inv_norm).astype(jnp.bfloat16)
-    return ((first_pre, first_act, second_pre, second_act, embedding, inv_norm), unit)
-
-
-def tower_backward(features, second, third, saved, unit_grad):
-    first_pre, first_act, second_pre, second_act, embedding, inv_norm = saved
-    along = jnp.sum(embedding * unit_grad, axis=1, keepdims=True)
-    embed_grad = (inv_norm * unit_grad - inv_norm * inv_norm * inv_norm * embedding * along).astype(
-        jnp.bfloat16
-    )
-    third_grad = contract_rows(second_act, embed_grad)
-    second_slope = (contract_cols(embed_grad, third) * silu_slope(second_pre)).astype(jnp.bfloat16)
-    second_grad = contract_rows(first_act, second_slope)
-    first_slope = (contract_cols(second_slope, second) * silu_slope(first_pre)).astype(jnp.bfloat16)
-    first_grad = contract_rows(features, first_slope)
-    return (first_grad, second_grad, third_grad)
+LOG2_E = 1.4426950408889634
 
 
 class Links:
@@ -315,7 +237,7 @@
         bufs[k] for k in ("c_in", "c_out", "y_in", "y_out", "z_in", "z_out")
     )
     c_out[0] = squares
-    c_out[1] = loss_tile[...]
+    c_out[1] = loss_tile
     f_own[...] = f_final
     s_own[...] = s_final
     t_own[...] = t_final
@@ -368,7 +290,7 @@
         o_third[t] = ag_third[t] * factor
 
 
-LINKS = 120
+LINKS = 192
 
 
 def ring_land(rows, cols):
@@ -411,37 +333,419 @@
 }
 
 
-def gradient_kernel(g_first, g_second, g_third, loss, o_first, o_second, o_third, o_loss, bufs, send, recv):
+Q_ROWS, P_ROWS, N_ROWS = pl.ds(0, 256), pl.ds(256, 256), pl.ds(512, 128)
+I_ROWS = pl.ds(256, 384)
+
+STEP_BUFS = {
+    "w1": pltpu.VMEM((2, 512, 1024), BF16),
+    "w2": pltpu.VMEM((2, 1024, 512), BF16),
+    "w3": pltpu.VMEM((2, 512, 256), BF16),
+    "x": pltpu.VMEM((640, 512), BF16),
+    "a1": pltpu.VMEM((640, 1024), BF16),
+    "a2": pltpu.VMEM((640, 512), BF16),
+    "s1": pltpu.VMEM((640, 1024), F32),
+    "s2": pltpu.VMEM((640, 512), F32),
+    "emb": pltpu.VMEM((640, 256), F32),
+    "inv": pltpu.VMEM((640, 1), F32),
+    "eg": pltpu.VMEM((640, 256), BF16),
+    "d2": pltpu.VMEM((640, 512), BF16),
+    "d1": pltpu.VMEM((640, 1024), BF16),
+    "xt": pltpu.VMEM((512, 640), BF16),
+    "a1t": pltpu.VMEM((1024, 640), BF16),
+    "a2t": pltpu.VMEM((512, 640), BF16),
+    "eye": pltpu.VMEM((256, 256), BF16),
+    "pos": pltpu.VMEM((256, 256), BF16),
+    "q": pltpu.VMEM((2048, 256), BF16),
+    "qs": pltpu.VMEM((2048, 256), BF16),
+    "n": pltpu.VMEM((2048, 256), BF16),
+    "nt": pltpu.VMEM((256, 2048), BF16),
+    "et": pltpu.VMEM((2048, 2048), BF16),
+    "turn": pltpu.VMEM((128, 128), F32),
+    "ids": pltpu.VMEM((2048, 128), F32),
+    "log": pltpu.VMEM((2048, 128), F32),
+    "part": pltpu.VMEM((8, 2048), F32),
+    "den_out": pltpu.VMEM((16, 128), F32),
+    "den_in": pltpu.VMEM((8, 16, 128), F32),
+    "den": pltpu.VMEM((16, 128), F32),
+    "p_out": pltpu.VMEM((2, 4, 256, 256), BF16),
+    "p_pair": pltpu.VMEM((4, 256, 256), BF16),
+    "p_ring": ring_land(256, 256),
+    "p_sum": pltpu.VMEM((256, 256), F32),
+    "g_out": pltpu.VMEM((2048, 256), BF16),
+    "g_ring": ring_land(512, 256),
+    "g_sum": pltpu.VMEM((512, 256), BF16),
+    "g_z": pltpu.VMEM((8, 64, 256), BF16),
+    "g_first": pltpu.VMEM((2, 512, 1024), BF16),
+    "g_second": pltpu.VMEM((2, 1024, 512), BF16),
+    "g_third": pltpu.VMEM((2, 4, 8, 16, 256), BF16),
+}
+
+
+def dot(a, b):
+    return jnp.dot(a, b, preferred_element_type=F32)
+
+
+def dot_cols(a, b):
+    return lax.dot_general(a, b, (((1,), (1,)), ((), ())), preferred_element_type=F32)
+
+
+def silu_both(pre):
+    sigma = 0.5 * jnp.tanh(0.5 * pre) + 0.5
+    act = pre * sigma
+    return act, sigma * (1.0 + pre - act)
+
+
+def forward(b, t, rows):
+    def layer(i, carry):
+        cols = pl.ds(multiple(i, 512), 512)
+        act, slope = silu_both(dot(b["x"][rows, :], b["w1"][t, :, cols]))
+        b["a1"][rows, cols] = act.astype(BF16)
+        b["s1"][rows, cols] = slope
+        return carry
+
+    lax.fori_loop(0, 2, layer, 0)
+    act, slope = silu_both(dot(b["a1"][rows, :], b["w2"][t]))
+    b["a2"][rows, :] = act.astype(BF16)
+    b["s2"][rows, :] = slope
+    embedding = dot(b["a2"][rows, :], b["w3"][t])
+    inv_norm = lax.rsqrt(jnp.sum(embedding * embedding, axis=1, keepdims=True) + 1.0)
+    b["emb"][rows, :] = embedding
+    b["inv"][rows, :] = inv_norm
+    return (embedding * inv_norm).astype(BF16)
+
+
+def backward(b, t, rows, unit_grad):
+    embedding, inv_norm = b["emb"][rows, :], b["inv"][rows, :]
+    along = jnp.sum(embedding * unit_grad, axis=1, keepdims=True)
+    embed_grad = inv_norm * unit_grad - inv_norm * inv_norm * inv_norm * embedding * along
+    b["eg"][rows, :] = embed_grad.astype(BF16)
+    slope = dot_cols(b["eg"][rows, :], b["w3"][t]) * b["s2"][rows, :]
+    b["d2"][rows, :] = slope.astype(BF16)
+
+    def layer(i, carry):
+        cols = pl.ds(multiple(i, 512), 512)
+        slope = dot_cols(b["d2"][rows, :], b["w2"][t, cols, :]) * b["s1"][rows, cols]
+        b["d1"][rows, cols] = slope.astype(BF16)
+        return carry
+
+    lax.fori_loop(0, 2, layer, 0)
+
+
+def weight_gradients(b, t, rows):
+    def first(i, carry):
+        cols = pl.ds(multiple(i, 512), 512)
+        b["g_first"][t, :, cols] = dot(b["xt"][:, rows], b["d1"][rows, cols]).astype(BF16)
+        return carry
+
+    lax.fori_loop(0, 2, first, 0)
+
+    def second(i, carry):
+        at = pl.ds(multiple(i, 512), 512)
+        b["g_second"][t, at, :] = dot(b["a1t"][at, rows], b["d2"][rows, :]).astype(BF16)
+        return carry
+
+    lax.fori_loop(0, 2, second, 0)
+    third = dot(b["a2t"][:, rows], b["eg"][rows, :]).astype(BF16)
+    b["g_third"][t] = third.reshape(4, 8, 16, 256)
+
+
+def turn_activations(b, rows):
+    for name, cols in (("x", 512), ("a1", 1024), ("a2", 512)):
+
+        def block(i, carry, name=name):
+            at = pl.ds(multiple(i, 256), 256)
+            turned = dot_cols(b["eye"][...], b[name][rows, at])
+            b[name + "t"][at, rows] = turned.astype(BF16)
+            return carry
+
+        lax.fori_loop(0, cols // 256, block, 0)
+
+
+def column(row):
+    return jnp.broadcast_to(row, (128, 128)).T
+
+
+def score_group(b, pos_ids, u):
+    at = pl.ds(multiple(u, 512), 512)
+    for h in range(2):
+        half = pl.ds(pl.multiple_of(u * 512 + h * 256, 256), 256)
+        b["nt"][:, half] = dot_cols(b["eye"][...], b["n"][half, :]).astype(BF16)
+
+    def block(i, carry):
+        cols = pl.ds(multiple(i, 512), 512)
+        products = dot_cols(b["n"][at, :], b["q"][cols, :])
+        logs = jnp.concatenate([b["log"][at, :]] * 4, axis=1)
+        ids = jnp.concatenate([b["ids"][at, :]] * 4, axis=1)
+        weights = jnp.exp2(products * (inv_temp * LOG2_E) - logs)
+        weights = jnp.where(pos_ids[:, cols] != ids, weights, 0.0)
+        b["et"][at, cols] = weights.astype(BF16)
+        b["part"][:, cols] += jnp.sum(weights.reshape(64, 8, 512), axis=0)
+        return carry
+
+    lax.fori_loop(0, 4, block, 0)
+
+
+def step_kernel(
+    query_x,
+    positive_x,
+    negative_x,
+    q1,
+    q2,
+    q3,
+    i1,
+    i2,
+    i3,
+    pos_ids,
+    pos_counts,
+    neg_ids,
+    neg_counts,
+    o_first,
+    o_second,
+    o_third,
+    o_loss,
+    b,
+    grad_bufs,
+    load,
+    send,
+    recv,
+):
+    y, z, x, c = (lax.axis_index(a) for a in (AX_Y, AX_Z, AX_X, AX_C))
+    me = x * 2 + c
     barrier, peers = greet_neighbours()
+    links = Links(send, recv, LINKS)
+
+    loads = [
+        (negative_x, b["x"].at[pl.ds(512, 64)]),
+        (i1, b["w1"].at[1]),
+        (i2, b["w2"].at[1]),
+        (i3, b["w3"].at[1]),
+        (query_x, b["x"].at[Q_ROWS]),
+        (q1, b["w1"].at[0]),
+        (q2, b["w2"].at[0]),
+        (q3, b["w3"].at[0]),
+        (positive_x, b["x"].at[P_ROWS]),
+    ]
+    loads = [pltpu.make_async_copy(s, d, load.at[k]) for k, (s, d) in enumerate(loads)]
+    for made in loads:
+        made.start()
+
+    b["x"][pl.ds(576, 64), :] = jnp.zeros((64, 512), BF16)
+    b["part"][...] = jnp.zeros((8, 2048), F32)
+    ones = lax.broadcasted_iota(jnp.int32, (256, 256), 0) == lax.broadcasted_iota(
+        jnp.int32, (256, 256), 1
+    )
+    b["eye"][...] = jnp.where(ones, 1.0, 0.0).astype(BF16)
+
+    for made in loads[:4]:
+        made.wait()
+    n = b["n"]
+    unit = forward(b, 1, N_ROWS)
+
+    def n_block(yy, zz):
+        return n.at[pl.ds(pl.multiple_of((yy * 8 + zz) * 64, 64), 64)]
+
+    def n_half(yy, zz, h):
+        return n.at[pl.ds(pl.multiple_of((yy * 8 + zz) * 64 + h * 32, 32), 32)]
+
+    n[pl.ds(pl.multiple_of((y * 8 + z) * 64, 64), 64), :] = unit[:64]
     pl.semaphore_wait(barrier, peers)
-    links = Links(send, recv, LINKS)
+    y_up, y_down = lax.rem(y + 1, 4), lax.rem(y + 3, 4)
+    order = (1, 7, 2, 6, 3, 5, 4)
+    n_z, n_y = {}, {}
+    for k in order:
+        n_z[k] = links.copy(n_block(y, z), n_block(y, z), {AX_Z: lax.rem(z + k, 8)})
+
+    def n_forward(k):
+        zz = lax.rem(z - k + 8, 8)
+        n_y[k] = (
+            links.copy(n_block(y, zz), n_block(y, zz), {AX_Y: y_up}),
+            links.copy(n_block(y, zz), n_block(y, zz), {AX_Y: y_down}),
+        )
+
+    n_forward(0)
+
+    for made in loads[4:8]:
+        made.wait()
+    q = b["q"]
+    q_own = forward(b, 0, Q_ROWS)
+
+    def q_block(xx, cc):
+        return q.at[pl.ds(pl.multiple_of((xx * 2 + cc) * 256, 256), 256)]
+
+    def q_half(xx, cc, h):
+        return q.at[pl.ds(pl.multiple_of((xx * 2 + cc) * 256 + h * 128, 128), 128)]
+
+    q[pl.ds(multiple(me, 256), 256), :] = q_own
+    x_up, x_down, x_far = lax.rem(x + 1, 4), lax.rem(x + 3, 4), lax.rem(x + 2, 4)
+    other = {AX_C: 1 - c}
+    q_up = links.copy(q_block(x, c), q_block(x, c), {AX_X: x_up})
+    q_down = links.copy(q_block(x, c), q_block(x, c), {AX_X: x_down})
+    q_pair = [links.copy(q_block(x, c), q_block(x, c), other)]
+
+    loads[8].wait()
+    b["pos"][...] = forward(b, 1, P_ROWS)
+
+    for k in order[:4]:
+        n_z[k].wait_recv()
+        n_forward(k)
+    q_up.wait_recv()
+    q_low = links.copy(q_half(x_down, c, 0), q_half(x_down, c, 0), {AX_X: x_up})
+    q_pair.append(links.copy(q_block(x_down, c), q_block(x_down, c), other))
+    q_down.wait_recv()
+    q_high = links.copy(q_half(x_up, c, 1), q_half(x_up, c, 1), {AX_X: x_down})
+    q_pair.append(links.copy(q_block(x_up, c), q_block(x_up, c), other))
+    for k in order[4:]:
+        n_z[k].wait_recv()
+        n_forward(k)
+
+    turn = b["turn"]
+    turn[...] = jnp.zeros((128, 128), F32)
+    turn[pl.ds(0, 16), :] = neg_ids[...].astype(F32)
+    turn[pl.ds(16, 16), :] = jnp.log(neg_counts[...].astype(F32)) * LOG2_E
+    turned = turn[...].T
+    for j in range(16):
+        b["ids"][pl.ds(j * 128, 128), :] = jnp.broadcast_to(turned[:, j : j + 1], (128, 128))
+        b["log"][pl.ds(j * 128, 128), :] = jnp.broadcast_to(
+            turned[:, 16 + j : 17 + j], (128, 128)
+        )
+
+    def n_relay(k):
+        zz = lax.rem(z - k + 8, 8)
+        from_down, from_up = n_y[k]
+        from_down.wait_recv()
+        low = links.copy(n_half(y_down, zz, 0), n_half(y_down, zz, 0), {AX_Y: y_up})
+        from_up.wait_recv()
+        high = links.copy(n_half(y_up, zz, 1), n_half(y_up, zz, 1), {AX_Y: y_down})
+        return (low, high)
+
+    n_far = []
+    for k in (0,) + order[:4]:
+        n_far.extend(n_relay(k))
+    q_low.wait_recv()
+    q_pair.append(links.copy(q_half(x_far, c, 0), q_half(x_far, c, 0), other))
+    q_high.wait_recv()
+    q_pair.append(links.copy(q_half(x_far, c, 1), q_half(x_far, c, 1), other))
+    for k in order[4:]:
+        n_far.extend(n_relay(k))
+    turn_activations(b, Q_ROWS)
+    turn_activations(b, P_ROWS)
+    turn_activations(b, N_ROWS)
+    for made in q_pair:
+        made.wait_recv()
+    score_group(b, pos_ids, y)
+    score_group(b, pos_ids, y_up)
+    score_group(b, pos_ids, y_down)
+
+    own = b["q"][pl.ds(multiple(me, 256), 256), :].astype(F32)
+    along = jnp.sum(own * b["pos"][...].astype(F32), axis=1, keepdims=True)
+    logits = []
+    for h in range(2):
+        row = jnp.broadcast_to(along[h * 128 : (h + 1) * 128], (128, 128)).T[0:1, :]
+        logits.append(row * inv_temp - jnp.log(pos_counts[h : h + 1, :].astype(F32)))
+
+    for made in n_far:
+        made.wait_recv()
+    score_group(b, pos_ids, lax.rem(y + 2, 4))
+
+    den_out, den_in = b["den_out"], b["den_in"]
+    for j in range(16):
+        den_out[pl.ds(j, 1), :] = jnp.sum(b["part"][:, j * 128 : (j + 1) * 128], axis=0, keepdims=True)
+    for h in range(2):
+        at = pl.ds(me * 2 + h, 1)
+        den_out[at, :] = den_out[at, :] + jnp.exp(logits[h])
+    group = []
+    for k in range(1, 8):
+        to = lax.rem(me + k, 8)
+        group.append({AX_X: to // 2, AX_C: lax.rem(to, 2)})
+    sums = [links.copy(den_out, den_in.at[me], peer) for peer in group]
+    den_in[me] = den_out[...]
+
+    p_out = b["p_out"]
+
+    def query_block(cc, i):
+        cols = pl.ds(pl.multiple_of((i * 2 + cc) * 256, 256), 256)
+        p_out[cc, i] = dot(b["nt"][...], b["et"][:, cols]).astype(BF16)
+
+    def theirs(i, carry):
+        query_block(1 - c, i)
+        return carry
+
+    def ours(i, carry):
+        query_block(c, i)
+        return carry
+
+    lax.fori_loop(0, 4, theirs, 0)
+    p_pair = b["p_pair"]
+    pair = links.copy(p_out.at[1 - c], p_pair, other)
+    for made in sums:
+        made.wait_recv()
+    total = den_in[0]
+    for j in range(1, 8):
+        total = total + den_in[j]
+    b["den"][...] = total
+    turn[pl.ds(0, 16), :] = 1.0 / total
+    turned = turn[...].T
+    for j in range(16):
+        at = pl.ds(j * 128, 128)
+        b["qs"][at, :] = (q[at, :].astype(F32) * turned[:, j : j + 1]).astype(BF16)
+
+    g_out = b["g_out"]
+
+    def negative_rows(u):
+        at = pl.ds(multiple(u, 512), 512)
+        g_out[at, :] = dot(b["et"][at, :], b["qs"][...]).astype(BF16)
+
+    g_y = Ring4(links, AX_Y, lambda j: g_out.at[pl.ds(multiple(j, 512), 512)], 512, b["g_ring"], 64)
+    negative_rows(g_y.far)
+    negative_rows(g_y.up)
+    negative_rows(g_y.down)
+    g_y.start()
+    negative_rows(g_y.me)
+    lax.fori_loop(0, 4, ours, 0)
+    pair.wait_recv()
+    for i in range(4):
+        add_rows(p_pair.at[i], (p_pair.at[i], p_out.at[c, i]), 256, 64)
+    p_x = Ring4(links, AX_X, lambda j: p_pair.at[j], 256, b["p_ring"], 128)
+    p_x.start()
+
+    losses, slopes, scales = [], [], []
+    for h in range(2):
+        den = b["den"][pl.ds(me * 2 + h, 1), :]
+        losses.append(jnp.log(den) - logits[h])
+        slope = column(jnp.exp(logits[h]) / den - 1.0) * inv_temp
+        slopes.append(jnp.concatenate([slope, slope], axis=1))
+        scale = column(inv_temp / den)
+        scales.append(jnp.concatenate([scale, scale], axis=1))
+    slopes = jnp.concatenate(slopes, axis=0)
+    scales = jnp.concatenate(scales, axis=0)
+    loss_tile = jnp.concatenate(losses + [jnp.zeros((6, 128), F32)], axis=0)
+    g_y.relay()
+    own = q[pl.ds(multiple(me, 256), 256), :].astype(F32)
+    backward(b, 1, P_ROWS, slopes * own)
+    p_x.relay()
+    g_sum = b["g_sum"]
+    g_y.end(g_sum)
+    g_z = Direct(links, AX_Z, 8, b["g_z"])
+    g_z.start(lambda j: g_sum.at[pl.ds(multiple(j, 64), 64)])
+
+    p_x.end(b["p_sum"])
+    query_grad = b["p_sum"][...].T * scales + slopes * b["pos"][...].astype(F32)
+    backward(b, 0, Q_ROWS, query_grad)
+    weight_gradients(b, 0, Q_ROWS)
+
+    g_z.wait()
+    total = g_sum[pl.ds(multiple(z, 64), 64), :].astype(F32)
+    for k in range(1, 8):
+        total = total + b["g_z"][lax.rem(z + k, 8)].astype(F32)
+    total = jnp.concatenate([total * inv_temp, jnp.zeros((64, 256), F32)], axis=0)
+    backward(b, 1, N_ROWS, total)
+    weight_gradients(b, 1, I_ROWS)
+
     outs = (o_first, o_second, o_third, o_loss)
-    reduce_gradients(links, g_first, g_second, g_third, loss, outs, bufs)
+    reduce_gradients(
+        links, b["g_first"], b["g_second"], b["g_third"], loss_tile, outs, grad_bufs
+    )
     links.finish()
-
-
-def reduced_gradients(g_first, g_second, g_third, loss):
-    vmem = pl.BlockSpec(memory_space=pltpu.VMEM)
-    return pl.pallas_call(
-        gradient_kernel,
-        out_shape=(
-            jax.ShapeDtypeStruct((2, 16, 1024), F32),
-            jax.ShapeDtypeStruct((2, 32, 512), F32),
-            jax.ShapeDtypeStruct((2, 16, 256), F32),
-            jax.ShapeDtypeStruct((8, 128), F32),
-        ),
-        in_specs=[vmem] * 4,
-        out_specs=(vmem,) * 4,
-        scratch_shapes=[
-            GRAD_BUFS,
-            pltpu.SemaphoreType.DMA((LINKS,)),
-            pltpu.SemaphoreType.DMA((LINKS,)),
-        ],
-        compiler_params=pltpu.CompilerParams(
-            collective_id=0, has_side_effects=True, vmem_limit_bytes=60 * 1024 * 1024
-        ),
-        name="reduce_gradients",
-    )(g_first, g_second, g_third, loss)
 
 
 def per_device(
@@ -459,58 +763,51 @@
     item_second,
     item_third,
 ):
-    own_rows = query_features.shape[0]
-    query_saved, query_unit = tower_forward(query_features, query_first, query_second, query_third)
-    item_features = jnp.concatenate([positive_features, negative_features], axis=0)
-    item_saved, item_unit = tower_forward(item_features, item_first, item_second, item_third)
-    positive_unit = item_unit[:own_rows]
-    negative_unit = item_unit[own_rows:]
-    group_unit = collect(query_unit, NEG, 0)
-    shard_unit = collect(negative_unit, DP, 0)
-    scores = (
-        contract_cols(group_unit, shard_unit) * inv_temp
-        - jnp.log(negative_counts.astype(jnp.float32))[None, :]
-    )
-    weights = jnp.where(positive_ids[:, None] != negative_ids[None, :], jnp.exp(scores), 0.0)
-    positive_logit = jnp.sum(
-        query_unit.astype(jnp.float32) * positive_unit.astype(jnp.float32), axis=1
-    ) * inv_temp - jnp.log(positive_counts.astype(jnp.float32))
-    positive_exp = jnp.exp(positive_logit)
-    offset = lax.axis_index(NEG) * own_rows
-    partial_value = jnp.sum(weights, axis=1)
-    own_part = lax.dynamic_slice(partial_value, (offset,), (own_rows,)) + positive_exp
-    partial_value = lax.dynamic_update_slice(partial_value, own_part, (offset,))
-    denom = over_copies(partial_value, NEG)
-    own_denom = lax.dynamic_slice(denom, (offset,), (own_rows,))
-    loss_part = jnp.sum(jnp.log(own_denom) - positive_logit)
-    softmax_weights = (weights / denom[:, None]).astype(jnp.bfloat16)
-    positive_slope = positive_exp / own_denom - 1.0
-    block = softmax_weights
-    query_sum = sent_and_summed(
-        jnp.dot(block, shard_unit, preferred_element_type=jnp.float32), NEG, 0
-    )
-    query_grad = (
-        query_sum + positive_slope[:, None] * positive_unit.astype(jnp.float32)
-    ) * inv_temp
-    block = softmax_weights
-    negative_sum = own_rows_2(contract_rows(block, group_unit), DP)
-    positive_grad = positive_slope[:, None] * query_unit.astype(jnp.float32) * inv_temp
-    item_grad = jnp.concatenate([positive_grad, negative_sum * inv_temp], axis=0)
-    query_grads = tower_backward(query_features, query_second, query_third, query_saved, query_grad)
-    item_grads = tower_backward(item_features, item_second, item_third, item_saved, item_grad)
-    stacked = [
-        jnp.stack([a.astype(BF16), b.astype(BF16)]) for a, b in zip(query_grads, item_grads)
-    ]
-    loss_tile = jnp.broadcast_to(loss_part * (1.0 / 1024.0), (8, 128))
-    first, second, third, loss = reduced_gradients(
-        stacked[0], stacked[1], stacked[2].reshape(2, 4, 8, 16, 256), loss_tile
-    )
-    mean_loss = loss[0, 0] / (own_rows * lax.axis_size(DP) * lax.axis_size(NEG))
+    vmem = pl.BlockSpec(memory_space=pltpu.VMEM)
+    anywhere = pl.BlockSpec(memory_space=pl.ANY)
+    first, second, third, loss = pl.pallas_call(
+        step_kernel,
+        out_shape=(
+            jax.ShapeDtypeStruct((2, 16, 1024), F32),
+            jax.ShapeDtypeStruct((2, 32, 512), F32),
+            jax.ShapeDtypeStruct((2, 16, 256), F32),
+            jax.ShapeDtypeStruct((8, 128), F32),
+        ),
+        in_specs=[anywhere] * 9 + [vmem] * 4,
+        out_specs=(vmem,) * 4,
+        scratch_shapes=[
+            STEP_BUFS,
+            GRAD_BUFS,
+            pltpu.SemaphoreType.DMA((9,)),
+            pltpu.SemaphoreType.DMA((LINKS,)),
+            pltpu.SemaphoreType.DMA((LINKS,)),
+        ],
+        compiler_params=pltpu.CompilerParams(
+            collective_id=0, has_side_effects=True, vmem_limit_bytes=62 * 1024 * 1024
+        ),
+        name="training_step",
+    )(
+        query_features,
+        positive_features,
+        negative_features,
+        query_first,
+        query_second,
+        query_third,
+        item_first,
+        item_second,
+        item_third,
+        positive_ids.astype(F32).reshape(1, 2048),
+        positive_counts.reshape(2, 128),
+        negative_ids.reshape(16, 128),
+        negative_counts.reshape(16, 128),
+    )
+    queries = query_features.shape[0] * lax.axis_size(DP) * lax.axis_size(NEG)
+    mean_loss = loss[0, 0] / queries
     return (mean_loss, first[0], second[0], third[0], first[1], second[1], third[1])
 
 
 def solution(mesh):
-    torus = Mesh(mesh.devices.reshape(4, 8, 4, 2), ("dp_0", "dp_1", "neg_0", "neg_1"))
+    torus = Mesh(mesh.devices.reshape(4, 8, 4, 2), DP_NEG)
     placed = (
         P(DP_NEG, None),
         P(DP_NEG, None),
@@ -530,14 +827,6 @@
         per_device,
         mesh=torus,
         in_specs=placed,
-        out_specs=(
-            P(),
-            P(DP, None),
-            P(DP, None),
-            P(DP, None),
-            P(DP, None),
-            P(DP, None),
-            P(DP, None),
-        ),
+        out_specs=(P(),) + (P(DP, None),) * 6,
         check_vma=False,
     )

time: 263 us -> 117 us (0.44)
  waiting for transfers between devices: 85.7 us -> 0 us
  Pallas kernels: 52.8 us -> 108 us
  matrix products: 38.3 us -> 0 us
  starting transfers between devices: 21.4 us -> 0 us
  other arithmetic: 19.8 us -> 1.3 us
  between operations: 16.8 us -> 2.43 us
  blocking collectives: 11.8 us -> 0 us
  local copies, waits for them, and re-layouts: 15.2 us -> 4.76 us
    all_to_all x3 -> x0, waiting for transfers between devices: 64.9 us -> none  [the longest x2 40 us: from_everyone(): return lax.all_to_all(copies, axis, split_axis=0, concat_axis=0, tiled=True)]
    pallas_call x1, Pallas kernels: 52.8 us -> 108 us  [per_device(): pl.pallas_call(step_kernel, out_shape=(jax.ShapeDtypeStruct((2, 16, 1024)...]
    dot_general x17 -> x0, matrix products: 38.3 us -> none  [the longest x7 13.4 us: contract_rows(): lax.dot_general(left, right, (((0,), (0,)), ((), ())), preferred_element_...]
    all_to_all x3 -> x0, starting transfers between devices: 21.4 us -> none  [the longest x2 17.1 us: from_everyone(): return lax.all_to_all(copies, axis, split_axis=0, concat_axis=0, tiled=True)]
    reduce_scatter x2 -> x0, waiting for transfers between devices: 20.8 us -> none  [own_rows_2(): so_far = lax.psum_scatter(so_far, axis, scatter_dimension=0, tiled=True)]
    all_to_all x1 -> x0, blocking collectives: 11.8 us -> none  [from_everyone(): return lax.all_to_all(copies, axis, split_axis=0, concat_axis=0, tiled=True)]
    convert_element_type x4 -> x1, other arithmetic: 10 us -> 1.3 us  [per_device(): positive_ids.astype(F32).reshape(1, 2048)]
    unnamed x59 -> x2, local copies, waits for them, and re-layouts: 6.79 us -> 0.01 us
  transfers between devices with their start and end apart: 5 -> 0, of which waited for: 4 -> 0; matrix products, arithmetic and copies ran while one was open for 7% -> 0% of each run, Pallas kernels for 0% -> 0%
where the time goes in v2:
time: 117 us
  Pallas kernels  108 us (92%)
  local copies, waits for them, and re-layouts  4.76 us (4%)
  between operations  2.43 us (2%)
  other arithmetic  1.3 us (1%)
    pallas_call x1, Pallas kernels, per_device(): pl.pallas_call(step_kernel, out_shape=(jax.ShapeDtypeStruct((2, 16, 1024)...  108 us

profile of v2, /device:TPU:1, one launch (start us, length us, event | category | flops | bytes accessed | tf_op | source)
XLA Modules:
  0.0 116.5 jit_solution(4620338485727990440)
XLA Ops:
  0.6 1.3 %convert_element_type.3 = f32[2048]{0:T(1024)} convert(s32[2048]{0:T(1024)} %param.16) | non-fusion elementwise | flops 2048 | bytes 16384 | tf_op jit(solution)/shard_map/convert_element_type | solution.py:799
  1.9 108.0 %training_step.1 = (f32[2,16,1024]{2,1,0:T(8,128)}, f32[2,32,512]{2,1,0:T(8,128)}, f32[2,16,256]{2,1,0:T(8,128)}, f32[8,128]{1,0:T(8,128)}) custom-call(bf16[256,512]{1,0:T(8,128)(2,1)} %query_x.1, bf16[256,512]{1,0:T(8,128)(2,1)} %positive_x.1, bf16[64,512]{1,0:T(8,128)(2,1)} %negative_x.1, bf16[512,1024]{1,0:T(8,128)(2,1)} %q1.1, bf16[1024,512]{1,0:T(8,128)(2,1)} %q2.1, ...), custom_call_target="tpu_custom_call" | custom-call | tf_op jit(solution)/shard_map/training_step/pallas_call | solution.py:768
  110.0 1.2 %slice.21 = f32[1,1]{1,0:T(1,128)} slice(f32[8,128]{1,0:T(8,128)} %get-tuple-element.11), slice={[0:1], [0:1]} | slice | bytes 8 | tf_op jit(solution)/shard_map/slice | solution.py:805
  111.8 1.3 %slice_bitcast_fusion.4 = (f32[16,256]{1,0:T(8,128)}, f32[16,256]{1,0:T(8,128)}) fusion(f32[2,16,256]{2,1,0:T(8,128)} %get-tuple-element.14), kind=kLoop, calls=%fused_computation.4 | loop fusion | bytes 65536 | tf_op jit(solution)/shard_map/squeeze | solution.py:806
  113.2 0.0 copy-start
  113.2 1.6 %slice_bitcast_fusion.1 = (f32[16,1024]{1,0:T(8,128)}, f32[16,1024]{1,0:T(8,128)}) fusion(f32[2,16,1024]{2,1,0:T(8,128)} %get-tuple-element.12), kind=kLoop, calls=%fused_computation.1 | loop fusion | bytes 262144 | tf_op jit(solution)/shard_map/squeeze | solution.py:806
  114.7 0.0 copy-done
  114.7 0.7 slice_bitcast_fusion
Async XLA Ops:
  113.2 1.6 %copy-start = (f32[2,32,512]{2,1,0:T(8,128)S(1)}, f32[2,32,512]{2,1,0:T(8,128)}, u32[]{:S(2)}) copy-start(f32[2,32,512]{2,1,0:T(8,128)} %get-tuple-element.13) | copy-start | bytes 393220

commit v3 on v2

v3 whole, which is shorter than its diff:
```python
import jax
import jax.numpy as jnp
from jax import lax
from jax.experimental import pallas as pl
from jax.experimental.pallas import tpu as pltpu
from jax.sharding import Mesh
from jax.sharding import PartitionSpec as P

NEG = ("neg_0", "neg_1")
DP = ("dp_0", "dp_1")
DP_NEG = ("dp_0", "dp_1", "neg_0", "neg_1")
NEG_DP = ("neg_0", "neg_1", "dp_0", "dp_1")
AX_Y, AX_Z, AX_X, AX_C = "dp_0", "dp_1", "neg_0", "neg_1"
MESH = pl.DeviceIdType.MESH
F32 = jnp.float32
BF16 = jnp.bfloat16

QUERIES = 65536
inv_temp = 20.0
clip_norm = 256.0
LOG2_E = 1.4426950408889634


class Links:
    def __init__(self, send_sems, recv_sems, size):
        self.send_sems, self.recv_sems, self.size = send_sems, recv_sems, size
        self.used = 0
        self.started = []

    def copy(self, src, dst, device):
        at = self.used
        self.used += 1
        assert at < self.size
        made = pltpu.make_async_remote_copy(
            src_ref=src,
            dst_ref=dst,
            send_sem=self.send_sems.at[at],
            recv_sem=self.recv_sems.at[at],
            device_id=device,
            device_id_type=MESH,
        )
        made.start()
        self.started.append(made)
        return made

    def finish(self):
        for made in self.started:
            made.wait_send()


def add_rows(out, terms, rows, step):
    def body(i, carry):
        at = pl.ds(pl.multiple_of(i * step, step), step)
        total = terms[0][at].astype(F32)
        for term in terms[1:]:
            total = total + term[at].astype(F32)
        out[at] = total.astype(out.dtype)
        return carry

    if rows == step:
        body(0, 0)
    else:
        lax.fori_loop(0, rows // step, body, 0)


class Phases:
    def __init__(self):
        self.scope = None

    def __call__(self, name):
        if self.scope is not None:
            self.scope.__exit__(None, None, None)
        self.scope = None
        if name is not None:
            self.scope = jax.named_scope(name)
            self.scope.__enter__()


class Ring4:
    def __init__(self, links, axis, cut, rows, land, step):
        self.links, self.axis, self.cut, self.rows, self.step = links, axis, cut, rows, step
        self.early_up, self.early_down, self.from_down, self.from_up = land
        me = lax.axis_index(axis)
        self.me = me
        self.up, self.down, self.far = lax.rem(me + 1, 4), lax.rem(me + 3, 4), lax.rem(me + 2, 4)
        half = rows // 2
        self.half, self.low, self.high = half, pl.ds(0, half), pl.ds(half, half)

    def start_far(self):
        far = self.cut(self.far)
        self.a = self.links.copy(far.at[self.low], self.early_up, {self.axis: self.up})
        self.b = self.links.copy(far.at[self.high], self.early_down, {self.axis: self.down})

    def start_near(self):
        self.c = self.links.copy(
            self.cut(self.up).at[self.high], self.from_down.at[self.high], {self.axis: self.up}
        )
        self.d = self.links.copy(
            self.cut(self.down).at[self.low], self.from_up.at[self.low], {self.axis: self.down}
        )

    def start(self):
        self.start_far()
        self.start_near()

    def relay(self):
        self.a.wait_recv()
        mine = self.cut(self.up).at[self.low]
        add_rows(self.early_up, (mine, self.early_up), self.half, self.step)
        self.e = self.links.copy(self.early_up, self.from_down.at[self.low], {self.axis: self.up})
        self.b.wait_recv()
        mine = self.cut(self.down).at[self.high]
        add_rows(self.early_down, (mine, self.early_down), self.half, self.step)
        self.f = self.links.copy(
            self.early_down, self.from_up.at[self.high], {self.axis: self.down}
        )

    def end(self, out):
        for made in (self.c, self.d, self.e, self.f):
            made.wait_recv()
        add_rows(out, (self.cut(self.me), self.from_down, self.from_up), self.rows, self.step)


class Direct:
    def __init__(self, links, axis, size, slots):
        self.links, self.axis, self.size, self.slots = links, axis, size, slots
        self.me = lax.axis_index(axis)

    def start(self, cut):
        self.made = []
        for k in range(1, self.size):
            to = lax.rem(self.me + k, self.size)
            self.made.append(self.links.copy(cut(to), self.slots.at[self.me], {self.axis: to}))

    def wait(self):
        for made in self.made:
            made.wait_recv()


def in_order(slots, count):
    total = slots[0].astype(F32)
    for j in range(1, count):
        total = total + slots[j].astype(F32)
    return total


def group_peers():
    x, c = lax.axis_index(AX_X), lax.axis_index(AX_C)
    peers = []
    for k in range(1, 8):
        other = lax.rem(x * 2 + c + k, 8)
        peers.append({AX_X: other // 2, AX_C: lax.rem(other, 2)})
    return peers


def plane_peers():
    y, z = lax.axis_index(AX_Y), lax.axis_index(AX_Z)
    peers = []
    for k in range(1, 32):
        other = lax.rem(y * 8 + z + k, 32)
        peers.append({AX_Y: other // 8, AX_Z: lax.rem(other, 8)})
    return peers


def greet_neighbours():
    barrier = pltpu.get_barrier_semaphore()
    peers = group_peers() + plane_peers()
    for peer in peers:
        pl.semaphore_signal(barrier, inc=1, device_id=peer, device_id_type=MESH)
    return barrier, len(peers)


def multiple(index, size):
    return pl.multiple_of(index * size, size)


class TowerSum:
    def __init__(self, links, b, g, t):
        self.links, self.b, self.t, self.g = links, b, t, g
        self.y, self.z, self.x, self.c = (lax.axis_index(a) for a in (AX_Y, AX_Z, AX_X, AX_C))

    def pair_first(self):
        columns = pl.ds(multiple(1 - self.c, 512), 512)
        mine = self.g["g_first"].at[self.t, :, :, columns]
        self.pair = [self.links.copy(mine, self.b["a_first"], {AX_C: 1 - self.c})]

    def pair_second(self):
        mine = self.g["g_second"].at[self.t, :, 1 - self.c]
        self.pair.append(self.links.copy(mine, self.b["a_second"], {AX_C: 1 - self.c}))

    def pair_third(self):
        columns = pl.ds(multiple(1 - self.c, 128), 128)
        mine = self.g["g_third"].at[self.t, :, :, :, columns]
        self.pair.append(self.links.copy(mine, self.b["a_third"], {AX_C: 1 - self.c}))

    def stage1(self):
        t, c, g, b, links = self.t, self.c, self.g, self.b, self.links
        first, second = b["a_first"], b["a_second"]
        self.pair[0].wait_recv()
        own = g["g_first"].at[t, :, :, pl.ds(multiple(c, 512), 512)]
        add_rows(first, (first, own), 32, 4)
        self.first_x = Ring4(
            links, AX_X, lambda j: first.at[:, :, pl.ds(multiple(j, 128), 128)], 32, b["fx"], 16
        )
        self.first_x.start()
        self.pair[1].wait_recv()
        add_rows(second, (second, g["g_second"].at[t, :, c]), 32, 4)
        self.second_y = Ring4(
            links, AX_Y, lambda j: second.at[pl.ds(multiple(j, 8), 8)], 8, b["sy"], 4
        )
        self.second_y.start()

    def third1(self):
        t, c, g, b, links = self.t, self.c, self.g, self.b, self.links
        third = b["a_third"]
        self.pair[2].wait_recv()
        own = g["g_third"].at[t, :, :, :, pl.ds(multiple(c, 128), 128)]
        add_rows(third, (third, own), 4, 1)
        self.third_z = Direct(links, AX_Z, 8, b["tz"])
        self.third_z.start(lambda j: third.at[:, j])

    def relay1(self):
        self.first_x.relay()
        self.second_y.relay()

    def third2(self):
        b = self.b
        self.third_z.wait()
        b["tz"][self.z] = b["a_third"][:, self.z]
        b["t_sum"][...] = in_order(b["tz"], 8).astype(BF16)
        self.third_y = Direct(self.links, AX_Y, 4, b["ty"])
        self.third_y.start(lambda j: b["t_sum"].at[j])

    def stage2(self):
        b, links = self.b, self.links
        fx_sum, sy_sum = b["fx_sum"], b["sy_sum"]
        self.first_x.end(fx_sum)
        self.first_y = Ring4(
            links, AX_Y, lambda j: fx_sum.at[pl.ds(multiple(j, 8), 8)], 8, b["fy"], 4
        )
        self.first_y.start()
        self.second_y.end(sy_sum)
        self.second_x = Ring4(
            links, AX_X, lambda j: sy_sum.at[:, :, pl.ds(multiple(j, 128), 128)], 8, b["sx"], 4
        )
        self.second_x.start()

    def third3(self):
        b = self.b
        self.third_y.wait()
        b["ty"][self.y] = b["t_sum"][self.y]
        b["ty_sum"][...] = in_order(b["ty"], 4).astype(BF16)
        self.third_x = Direct(self.links, AX_X, 4, b["tx"])
        self.third_x.start(lambda j: b["ty_sum"])

    def relay2(self):
        self.first_y.relay()
        self.second_x.relay()

    def stage3(self):
        b = self.b
        both = b["both"]
        self.first_y.end(both.at[:, 0])
        self.second_x.end(both.at[:, 1])
        self.last_z = Direct(self.links, AX_Z, 8, b["lz"])
        self.last_z.start(lambda j: both.at[j])

    def last(self):
        b, t = self.b, self.t
        self.third_x.wait()
        b["tx"][self.x] = b["ty_sum"][...]
        third = in_order(b["tx"], 4)
        self.last_z.wait()
        b["lz"][self.z] = b["both"][self.z]
        piece = in_order(b["lz"], 8)
        b["own"][...] = piece
        b["t_own"][...] = third
        squares = jnp.sum((piece * piece).reshape(4, 8, 128), axis=0)
        return squares + jnp.sum((third * third).reshape(2, 8, 128), axis=0) * 0.25

    def spread(self):
        b, me = self.b, self.x * 2 + self.c
        self.pieces = [self.links.copy(b["t_own"], b["ag_third"].at[self.c], {AX_C: 1 - self.c})]
        for peer in group_peers():
            self.pieces.append(self.links.copy(b["own"], b["ag"].at[me], peer))
        b["ag"][me] = b["own"][...]
        b["ag_third"][self.c] = b["t_own"][...]

    def collect(self, o_first, o_second, o_third):
        b = self.b
        for made in self.pieces:
            made.wait_recv()
        for cc in range(2):
            for xx in range(4):
                me = xx * 2 + cc
                o_first[:, pl.ds(cc * 512 + xx * 128, 128)] = b["ag"][me, 0]
                o_second[pl.ds(cc * 16, 16), pl.ds(xx * 128, 128)] = b["ag"][me, 1]
            o_third[:, pl.ds(cc * 128, 128)] = b["ag_third"][cc]


LINKS = 256


def ring_land(rows, *rest):
    half = pltpu.VMEM((rows // 2, *rest), BF16)
    whole = pltpu.VMEM((rows, *rest), BF16)
    return (half, half, whole, whole)


SUM_BUFS = {
    "a_first": pltpu.VMEM((32, 16, 512), BF16),
    "a_second": pltpu.VMEM((32, 16, 512), BF16),
    "a_third": pltpu.VMEM((4, 8, 16, 128), BF16),
    "fx": ring_land(32, 16, 128),
    "sy": ring_land(8, 16, 512),
    "tz": pltpu.VMEM((8, 4, 16, 128), BF16),
    "t_sum": pltpu.VMEM((4, 16, 128), BF16),
    "ty": pltpu.VMEM((4, 16, 128), BF16),
    "ty_sum": pltpu.VMEM((16, 128), BF16),
    "tx": pltpu.VMEM((4, 16, 128), BF16),
    "fx_sum": pltpu.VMEM((32, 16, 128), BF16),
    "sy_sum": pltpu.VMEM((8, 16, 512), BF16),
    "fy": ring_land(8, 16, 128),
    "sx": ring_land(8, 16, 128),
    "both": pltpu.VMEM((8, 2, 16, 128), BF16),
    "lz": pltpu.VMEM((8, 2, 16, 128), BF16),
    "own": pltpu.VMEM((2, 16, 128), F32),
    "t_own": pltpu.VMEM((16, 128), F32),
    "ag": pltpu.VMEM((8, 2, 16, 128), F32),
    "ag_third": pltpu.VMEM((2, 16, 128), F32),
}

SCALAR_BUFS = {
    "c_in": pltpu.VMEM((8, 8, 128), F32),
    "c_out": pltpu.VMEM((8, 128), F32),
    "p_in": pltpu.VMEM((32, 8, 128), F32),
    "p_out": pltpu.VMEM((8, 128), F32),
    "total": pltpu.VMEM((8, 128), F32),
}


ROWS = pl.ds(0, 4)


class Scalars:
    def __init__(self, links, b):
        self.links, self.b = links, b

    def start(self, squares):
        b, links = self.b, self.links
        me = lax.axis_index(AX_X) * 2 + lax.axis_index(AX_C)
        b["c_out"][0:1] = jnp.sum(squares, axis=0, keepdims=True)
        self.made = [links.copy(b["c_out"].at[ROWS], b["c_in"].at[me, ROWS], peer) for peer in group_peers()]
        b["c_in"][me, ROWS] = b["c_out"][ROWS]

    def over_plane(self):
        b, links = self.b, self.links
        d = lax.axis_index(AX_Y) * 8 + lax.axis_index(AX_Z)
        for made in self.made:
            made.wait_recv()
        b["p_out"][ROWS] = in_order(b["c_in"].at[:, ROWS], 8)
        self.made = [links.copy(b["p_out"].at[ROWS], b["p_in"].at[d, ROWS], peer) for peer in plane_peers()]
        b["p_in"][d, ROWS] = b["p_out"][ROWS]

    def end(self):
        for made in self.made:
            made.wait_recv()
        self.b["total"][ROWS] = in_order(self.b["p_in"].at[:, ROWS], 32)
        return self.b["total"][...]


Q_ROWS, P_ROWS, N_ROWS = pl.ds(0, 256), pl.ds(256, 256), pl.ds(512, 128)
I_ROWS = pl.ds(256, 384)

STEP_BUFS = {
    "pos_ids": pltpu.VMEM((16, 128), jnp.int32),
    "pos_counts": pltpu.VMEM((2, 128), jnp.int32),
    "neg_ids": pltpu.VMEM((16, 128), jnp.int32),
    "neg_counts": pltpu.VMEM((16, 128), jnp.int32),
    "w1": pltpu.VMEM((2, 512, 1024), BF16),
    "w2": pltpu.VMEM((2, 1024, 512), BF16),
    "w3": pltpu.VMEM((2, 512, 256), BF16),
    "x": pltpu.VMEM((640, 512), BF16),
    "a1": pltpu.VMEM((640, 1024), BF16),
    "a2": pltpu.VMEM((640, 512), BF16),
    "s1": pltpu.VMEM((640, 1024), F32),
    "s2": pltpu.VMEM((640, 512), F32),
    "emb": pltpu.VMEM((640, 256), F32),
    "inv": pltpu.VMEM((640, 1), F32),
    "eg": pltpu.VMEM((640, 256), BF16),
    "d2": pltpu.VMEM((640, 512), BF16),
    "d1": pltpu.VMEM((640, 1024), BF16),
    "xt": pltpu.VMEM((512, 640), BF16),
    "a1t": pltpu.VMEM((1024, 640), BF16),
    "a2t": pltpu.VMEM((512, 640), BF16),
    "eye": pltpu.VMEM((256, 256), BF16),
    "pos": pltpu.VMEM((256, 256), BF16),
    "q": pltpu.VMEM((2048, 256), BF16),
    "qs": pltpu.VMEM((2048, 256), BF16),
    "n": pltpu.VMEM((2048, 256), BF16),
    "nt": pltpu.VMEM((256, 2048), BF16),
    "et": pltpu.VMEM((2048, 2048), BF16),
    "turn": pltpu.VMEM((128, 128), F32),
    "ids": pltpu.VMEM((2048, 128), F32),
    "log": pltpu.VMEM((2048, 128), F32),
    "part": pltpu.VMEM((8, 2048), F32),
    "den_out": pltpu.VMEM((16, 128), F32),
    "den_in": pltpu.VMEM((8, 16, 128), F32),
    "den": pltpu.VMEM((16, 128), F32),
    "p_out": pltpu.VMEM((2, 4, 256, 256), BF16),
    "p_pair": pltpu.VMEM((4, 256, 256), BF16),
    "p_ring": ring_land(256, 256),
    "p_sum": pltpu.VMEM((256, 256), F32),
    "g_out": pltpu.VMEM((2048, 256), BF16),
    "g_ring": ring_land(512, 256),
    "g_sum": pltpu.VMEM((512, 256), BF16),
    "g_z": pltpu.VMEM((8, 64, 256), BF16),
    "g_first": pltpu.VMEM((2, 32, 16, 1024), BF16),
    "g_second": pltpu.VMEM((2, 32, 2, 16, 512), BF16),
    "g_third": pltpu.VMEM((2, 4, 8, 16, 256), BF16),
    "sum_query": SUM_BUFS,
    "sum_item": SUM_BUFS,
    "scalars": SCALAR_BUFS,
}


def dot(a, b):
    return jnp.dot(a, b, preferred_element_type=F32)


def dot_cols(a, b):
    return lax.dot_general(a, b, (((1,), (1,)), ((), ())), preferred_element_type=F32)


def silu_both(pre):
    sigma = 0.5 * jnp.tanh(0.5 * pre) + 0.5
    act = pre * sigma
    return act, sigma * (1.0 + pre - act)


def forward(b, t, rows, loads=()):
    def layer(i, carry):
        cols = pl.ds(multiple(i, 512), 512)
        act, slope = silu_both(dot(b["x"][rows, :], b["w1"][t, :, cols]))
        b["a1"][rows, cols] = act.astype(BF16)
        b["s1"][rows, cols] = slope
        return carry

    lax.fori_loop(0, 2, layer, 0)
    for made in loads:
        made.wait()
    act, slope = silu_both(dot(b["a1"][rows, :], b["w2"][t]))
    b["a2"][rows, :] = act.astype(BF16)
    b["s2"][rows, :] = slope
    embedding = dot(b["a2"][rows, :], b["w3"][t])
    inv_norm = lax.rsqrt(jnp.sum(embedding * embedding, axis=1, keepdims=True) + 1.0)
    b["emb"][rows, :] = embedding
    b["inv"][rows, :] = inv_norm
    return (embedding * inv_norm).astype(BF16)


def backward(b, t, rows, unit_grad):
    embedding, inv_norm = b["emb"][rows, :], b["inv"][rows, :]
    along = jnp.sum(embedding * unit_grad, axis=1, keepdims=True)
    embed_grad = inv_norm * unit_grad - inv_norm * inv_norm * inv_norm * embedding * along
    b["eg"][rows, :] = embed_grad.astype(BF16)
    slope = dot_cols(b["eg"][rows, :], b["w3"][t]) * b["s2"][rows, :]
    b["d2"][rows, :] = slope.astype(BF16)

    def layer(i, carry):
        cols = pl.ds(multiple(i, 512), 512)
        slope = dot_cols(b["d2"][rows, :], b["w2"][t, cols, :]) * b["s1"][rows, cols]
        b["d1"][rows, cols] = slope.astype(BF16)
        return carry

    lax.fori_loop(0, 2, layer, 0)


def weight_gradients(b, t, rows, tower):
    def first(i, carry):
        cols = pl.ds(multiple(i, 512), 512)
        made = dot(b["xt"][:, rows], b["d1"][rows, cols]).astype(BF16)
        b["g_first"][t, :, :, cols] = made.reshape(32, 16, 512)
        return carry

    lax.fori_loop(0, 2, first, 0)
    tower.pair_first()

    def second(i, carry):
        at = pl.ds(multiple(i, 512), 512)
        made = dot(b["a1t"][at, rows], b["d2"][rows, :]).astype(BF16)
        b["g_second"][t, pl.ds(multiple(i, 16), 16)] = made.reshape(16, 2, 16, 512)
        return carry

    lax.fori_loop(0, 2, second, 0)
    tower.pair_second()
    third = dot(b["a2t"][:, rows], b["eg"][rows, :]).astype(BF16)
    b["g_third"][t] = third.reshape(4, 8, 16, 256)
    tower.pair_third()


def turn_activations(b, rows):
    for name, cols in (("x", 512), ("a1", 1024), ("a2", 512)):

        def block(i, carry, name=name):
            at = pl.ds(multiple(i, 256), 256)
            turned = dot_cols(b["eye"][...], b[name][rows, at])
            b[name + "t"][at, rows] = turned.astype(BF16)
            return carry

        lax.fori_loop(0, cols // 256, block, 0)


def column(row):
    return jnp.broadcast_to(row, (128, 128)).T


def turn_negatives(b, u):
    for h in range(2):
        half = pl.ds(pl.multiple_of(u * 512 + h * 256, 256), 256)
        b["nt"][:, half] = dot_cols(b["eye"][...], b["n"][half, :]).astype(BF16)


def score_tile(b, pos_ids, u, i):
    at, cols = pl.ds(multiple(u, 512), 512), pl.ds(multiple(i, 512), 512)
    products = dot_cols(b["n"][at, :], b["q"][cols, :])
    logs = jnp.concatenate([b["log"][at, :]] * 4, axis=1)
    ids = jnp.concatenate([b["ids"][at, :]] * 4, axis=1)
    weights = jnp.exp2(products * (inv_temp * LOG2_E) - logs)
    rows = [pos_ids[pl.ds(i * 4 + r, 1), :].astype(F32) for r in range(4)]
    weights = jnp.where(jnp.concatenate(rows, axis=1) != ids, weights, 0.0)
    b["et"][at, cols] = weights.astype(BF16)
    b["part"][:, cols] += jnp.sum(weights.reshape(64, 8, 512), axis=0)


def step_kernel(
    query_x,
    positive_x,
    negative_x,
    q1,
    q2,
    q3,
    i1,
    i2,
    i3,
    pos_ids_in,
    pos_counts_in,
    neg_ids_in,
    neg_counts_in,
    o_query_first,
    o_query_second,
    o_query_third,
    o_item_first,
    o_item_second,
    o_item_third,
    o_scalars,
    b,
    load,
    send,
    recv,
):
    y, z, x, c = (lax.axis_index(a) for a in (AX_Y, AX_Z, AX_X, AX_C))
    me = x * 2 + c
    barrier, peers = greet_neighbours()
    links = Links(send, recv, LINKS)
    phase = Phases()
    phase("load")

    loads = [
        (negative_x, b["x"].at[pl.ds(512, 64)]),
        (i1, b["w1"].at[1]),
        (i2, b["w2"].at[1]),
        (i3, b["w3"].at[1]),
        (query_x, b["x"].at[Q_ROWS]),
        (q1, b["w1"].at[0]),
        (q2, b["w2"].at[0]),
        (q3, b["w3"].at[0]),
        (positive_x, b["x"].at[P_ROWS]),
        (pos_ids_in, b["pos_ids"]),
        (pos_counts_in, b["pos_counts"]),
        (neg_ids_in, b["neg_ids"]),
        (neg_counts_in, b["neg_counts"]),
    ]
    loads = [pltpu.make_async_copy(s, d, load.at[k]) for k, (s, d) in enumerate(loads)]
    for made in loads:
        made.start()

    b["x"][pl.ds(576, 64), :] = jnp.zeros((64, 512), BF16)
    b["part"][...] = jnp.zeros((8, 2048), F32)
    b["scalars"]["c_out"][...] = jnp.zeros((8, 128), F32)
    b["scalars"]["total"][...] = jnp.zeros((8, 128), F32)
    ones = lax.broadcasted_iota(jnp.int32, (256, 256), 0) == lax.broadcasted_iota(
        jnp.int32, (256, 256), 1
    )
    b["eye"][...] = jnp.where(ones, 1.0, 0.0).astype(BF16)

    loads[0].wait()
    loads[1].wait()
    phase("f_neg")
    n = b["n"]
    unit = forward(b, 1, N_ROWS, loads[2:4])

    def n_block(yy, zz):
        return n.at[pl.ds(pl.multiple_of((yy * 8 + zz) * 64, 64), 64)]

    def n_half(yy, zz, h):
        return n.at[pl.ds(pl.multiple_of((yy * 8 + zz) * 64 + h * 32, 32), 32)]

    n[pl.ds(pl.multiple_of((y * 8 + z) * 64, 64), 64), :] = unit[:64]
    phase("barrier")
    pl.semaphore_wait(barrier, peers)
    y_up, y_down = lax.rem(y + 1, 4), lax.rem(y + 3, 4)
    order = (1, 7, 2, 6, 3, 5, 4)
    n_z, n_y = {}, {}
    for k in order:
        n_z[k] = links.copy(n_block(y, z), n_block(y, z), {AX_Z: lax.rem(z + k, 8)})

    def n_forward(k):
        zz = lax.rem(z - k + 8, 8)
        n_y[k] = (
            links.copy(n_block(y, zz), n_block(y, zz), {AX_Y: y_up}),
            links.copy(n_block(y, zz), n_block(y, zz), {AX_Y: y_down}),
        )

    n_forward(0)

    phase("f_query")
    for made in loads[4:8]:
        made.wait()
    q = b["q"]
    q_own = forward(b, 0, Q_ROWS)

    def q_block(xx, cc):
        return q.at[pl.ds(pl.multiple_of((xx * 2 + cc) * 256, 256), 256)]

    def q_half(xx, cc, h):
        return q.at[pl.ds(pl.multiple_of((xx * 2 + cc) * 256 + h * 128, 128), 128)]

    q[pl.ds(multiple(me, 256), 256), :] = q_own
    x_up, x_down, x_far = lax.rem(x + 1, 4), lax.rem(x + 3, 4), lax.rem(x + 2, 4)
    other = {AX_C: 1 - c}
    q_up = links.copy(q_block(x, c), q_block(x, c), {AX_X: x_up})
    q_down = links.copy(q_block(x, c), q_block(x, c), {AX_X: x_down})
    q_pair = [links.copy(q_block(x, c), q_block(x, c), other)]

    phase("f_pos")
    for made in loads[8:]:
        made.wait()
    pos_ids, pos_counts, neg_ids, neg_counts = (
        b[k] for k in ("pos_ids", "pos_counts", "neg_ids", "neg_counts")
    )
    b["pos"][...] = forward(b, 1, P_ROWS)

    phase("n_fwd1")
    for k in order[:4]:
        n_z[k].wait_recv()
        n_forward(k)
    phase("q_relay")
    q_up.wait_recv()
    q_low = links.copy(q_half(x_down, c, 0), q_half(x_down, c, 0), {AX_X: x_up})
    q_pair.append(links.copy(q_block(x_down, c), q_block(x_down, c), other))
    q_down.wait_recv()
    q_high = links.copy(q_half(x_up, c, 1), q_half(x_up, c, 1), {AX_X: x_down})
    q_pair.append(links.copy(q_block(x_up, c), q_block(x_up, c), other))

    phase("small")
    turn = b["turn"]
    turn[...] = jnp.zeros((128, 128), F32)
    turn[pl.ds(0, 16), :] = neg_ids[...].astype(F32)
    turn[pl.ds(16, 16), :] = jnp.log(neg_counts[...].astype(F32)) * LOG2_E
    turned = turn[...].T
    for j in range(16):
        b["ids"][pl.ds(j * 128, 128), :] = jnp.broadcast_to(turned[:, j : j + 1], (128, 128))
        b["log"][pl.ds(j * 128, 128), :] = jnp.broadcast_to(
            turned[:, 16 + j : 17 + j], (128, 128)
        )
    phase("n_fwd2")
    for k in order[4:]:
        n_z[k].wait_recv()
        n_forward(k)

    n_far = []

    def n_relay(*which):
        for k in which:
            zz = lax.rem(z - k + 8, 8)
            from_down, from_up = n_y[k]
            from_down.wait_recv()
            n_far.append(
                links.copy(n_half(y_down, zz, 0), n_half(y_down, zz, 0), {AX_Y: y_up})
            )
            from_up.wait_recv()
            n_far.append(
                links.copy(n_half(y_up, zz, 1), n_half(y_up, zz, 1), {AX_Y: y_down})
            )

    phase("relay_a")
    n_relay(0, 1, 7)
    q_pair[0].wait_recv()
    phase("tile_a")
    score_tile(b, pos_ids, y, x)
    phase("relay_b")
    n_relay(2, 6)
    q_pair[1].wait_recv()
    phase("tile_b")
    score_tile(b, pos_ids, y, x_down)
    phase("relay_c")
    q_low.wait_recv()
    q_pair.append(links.copy(q_half(x_far, c, 0), q_half(x_far, c, 0), other))
    q_high.wait_recv()
    q_pair.append(links.copy(q_half(x_far, c, 1), q_half(x_far, c, 1), other))
    n_relay(3, 5)
    q_pair[2].wait_recv()
    phase("tile_c")
    score_tile(b, pos_ids, y, x_up)
    phase("relay_d")
    n_relay(4)
    phase("tiles")
    for made in q_pair[3:]:
        made.wait_recv()
    score_tile(b, pos_ids, y, x_far)

    def near_tiles(i, carry):
        score_tile(b, pos_ids, y_up, i)
        score_tile(b, pos_ids, y_down, i)
        return carry

    lax.fori_loop(0, 4, near_tiles, 0)
    phase("logits")
    own = b["q"][pl.ds(multiple(me, 256), 256), :].astype(F32)
    along = jnp.sum(own * b["pos"][...].astype(F32), axis=1, keepdims=True)
    logits = []
    for h in range(2):
        row = jnp.broadcast_to(along[h * 128 : (h + 1) * 128], (128, 128)).T[0:1, :]
        logits.append(row * inv_temp - jnp.log(pos_counts[h : h + 1, :].astype(F32)))

    phase("n_far")
    for made in n_far:
        made.wait_recv()
    phase("far_tiles")
    y_far = lax.rem(y + 2, 4)

    def far_tiles(i, carry):
        score_tile(b, pos_ids, y_far, i)
        return carry

    lax.fori_loop(0, 4, far_tiles, 0)

    phase("den")
    den_out, den_in = b["den_out"], b["den_in"]
    for j in range(16):
        den_out[pl.ds(j, 1), :] = jnp.sum(b["part"][:, j * 128 : (j + 1) * 128], axis=0, keepdims=True)
    for h in range(2):
        at = pl.ds(me * 2 + h, 1)
        den_out[at, :] = den_out[at, :] + jnp.exp(logits[h])
    sums = [links.copy(den_out, den_in.at[me], peer) for peer in group_peers()]
    den_in[me] = den_out[...]

    def turned(u, carry):
        turn_negatives(b, u)
        return carry

    lax.fori_loop(0, 4, turned, 0)

    phase("p_theirs")
    p_out = b["p_out"]

    def query_block(cc, i):
        cols = pl.ds(pl.multiple_of((i * 2 + cc) * 256, 256), 256)
        p_out[cc, i] = dot(b["nt"][...], b["et"][:, cols]).astype(BF16)

    def theirs(i, carry):
        query_block(1 - c, i)
        return carry

    def ours(i, carry):
        query_block(c, i)
        return carry

    lax.fori_loop(0, 4, theirs, 0)
    p_pair = b["p_pair"]
    pair = links.copy(p_out.at[1 - c], p_pair, other)
    phase("p_ours")
    lax.fori_loop(0, 4, ours, 0)
    phase("p_add")
    pair.wait_recv()
    for i in range(4):
        add_rows(p_pair.at[i], (p_pair.at[i], p_out.at[c, i]), 256, 64)
    p_x = Ring4(links, AX_X, lambda j: p_pair.at[j], 256, b["p_ring"], 128)
    p_x.start()

    phase("den_wait")
    for made in sums:
        made.wait_recv()
    total = in_order(den_in, 8)
    b["den"][...] = total
    turn[pl.ds(0, 16), :] = 1.0 / total
    turned = turn[...].T
    for j in range(16):
        at = pl.ds(j * 128, 128)
        b["qs"][at, :] = (q[at, :].astype(F32) * turned[:, j : j + 1]).astype(BF16)

    phase("g_rows")
    g_out = b["g_out"]

    def negative_rows(u):
        at = pl.ds(multiple(u, 512), 512)
        g_out[at, :] = dot(b["et"][at, :], b["qs"][...]).astype(BF16)

    g_y = Ring4(links, AX_Y, lambda j: g_out.at[pl.ds(multiple(j, 512), 512)], 512, b["g_ring"], 64)
    negative_rows(g_y.far)
    g_y.start_far()
    negative_rows(g_y.up)
    negative_rows(g_y.down)
    g_y.start_near()
    phase("p_relay")
    p_x.relay()
    phase("g_own")
    negative_rows(g_y.me)

    phase("slopes")
    losses, slopes, scales = [], [], []
    for h in range(2):
        den = b["den"][pl.ds(me * 2 + h, 1), :]
        losses.append(jnp.log(den) - logits[h])
        slope = column(jnp.exp(logits[h]) / den - 1.0) * inv_temp
        slopes.append(jnp.concatenate([slope, slope], axis=1))
        scale = column(inv_temp / den)
        scales.append(jnp.concatenate([scale, scale], axis=1))
    slopes = jnp.concatenate(slopes, axis=0)
    scales = jnp.concatenate(scales, axis=0)
    for h in range(2):
        b["scalars"]["c_out"][h + 1 : h + 2] = losses[h]
    phase("b_pos")
    own = q[pl.ds(multiple(me, 256), 256), :].astype(F32)
    backward(b, 1, P_ROWS, slopes * own)
    phase("g_relay")
    g_y.relay()
    phase("turn_q")
    turn_activations(b, Q_ROWS)

    phase("p_end")
    p_x.end(b["p_sum"])
    query_grad = b["p_sum"][...].T * scales + slopes * b["pos"][...].astype(F32)
    phase("b_query")
    backward(b, 0, Q_ROWS, query_grad)
    phase("w_query")
    query_sum = TowerSum(links, b["sum_query"], b, 0)
    item_sum = TowerSum(links, b["sum_item"], b, 1)
    weight_gradients(b, 0, Q_ROWS, query_sum)
    phase("g_end")
    g_sum = b["g_sum"]
    g_y.end(g_sum)
    g_z = Direct(links, AX_Z, 8, b["g_z"])
    g_z.start(lambda j: g_sum.at[pl.ds(multiple(j, 64), 64)])

    phase("q_stage1")
    query_sum.stage1()
    phase("turn_p")
    turn_activations(b, P_ROWS)
    phase("q_relay1")
    query_sum.relay1()
    phase("turn_n")
    turn_activations(b, N_ROWS)

    phase("g_z")
    g_z.wait()
    total = g_sum[pl.ds(multiple(z, 64), 64), :].astype(F32)
    for k in range(1, 8):
        total = total + b["g_z"][lax.rem(z + k, 8)].astype(F32)
    total = jnp.concatenate([total * inv_temp, jnp.zeros((64, 256), F32)], axis=0)
    phase("b_neg")
    backward(b, 1, N_ROWS, total)
    phase("q_stage2")
    query_sum.stage2()
    query_sum.third1()
    phase("w_item")
    weight_gradients(b, 1, I_ROWS, item_sum)
    phase("q_relay2")
    query_sum.relay2()
    phase("i_stage1")
    item_sum.stage1()
    item_sum.third1()
    phase("q_third2")
    query_sum.third2()
    phase("q_stage3")
    query_sum.stage3()
    phase("i_relay1")
    item_sum.relay1()
    phase("i_stage2")
    item_sum.stage2()
    phase("q_third3")
    query_sum.third3()
    item_sum.third2()
    phase("i_relay2")
    item_sum.relay2()
    item_sum.third3()
    phase("q_last")
    squares = query_sum.last()
    query_sum.spread()
    phase("i_stage3")
    item_sum.stage3()
    phase("i_last")
    squares = squares + item_sum.last()
    scalars = Scalars(links, b["scalars"])
    scalars.start(squares)
    item_sum.spread()
    phase("group")
    scalars.over_plane()
    phase("plane")
    total = scalars.end()
    row = lax.broadcasted_iota(jnp.int32, (8, 128), 0)
    norm = jnp.sqrt(jnp.sum(jnp.where(row == 0, total, 0.0), keepdims=True))
    factor = clip_norm / jnp.maximum(norm, clip_norm)
    o_scalars[0] = jnp.broadcast_to(factor, (8, 128))
    o_scalars[1] = jnp.broadcast_to(jnp.sum(jnp.where((row == 1) | (row == 2), total, 0.0), keepdims=True), (8, 128))
    phase("pieces")
    query_sum.collect(o_query_first, o_query_second, o_query_third)
    item_sum.collect(o_item_first, o_item_second, o_item_third)
    phase("finish")
    links.finish()
    phase(None)


def clip_kernel(*refs):
    scalars, raw, clipped, loss = refs[0], refs[1:7], refs[7:13], refs[13]
    factor = scalars[0, 0:1, 0:1]
    for source, result in zip(raw, clipped):
        result[...] = source[...] * factor
    loss[...] = scalars[1, 0:1, 0:1] * (1.0 / QUERIES)


def per_device(
    query_features,
    positive_features,
    negative_features,
    positive_ids,
    positive_counts,
    negative_ids,
    negative_counts,
    query_first,
    query_second,
    query_third,
    item_first,
    item_second,
    item_third,
):
    vmem = pl.BlockSpec(memory_space=pltpu.VMEM)
    anywhere = pl.BlockSpec(memory_space=pl.ANY)
    tower = (
        jax.ShapeDtypeStruct((16, 1024), F32),
        jax.ShapeDtypeStruct((32, 512), F32),
        jax.ShapeDtypeStruct((16, 256), F32),
    )
    *raw, scalars = pl.pallas_call(
        step_kernel,
        out_shape=tower + tower + (jax.ShapeDtypeStruct((2, 8, 128), F32),),
        in_specs=[anywhere] * 13,
        out_specs=(vmem,) * 7,
        scratch_shapes=[
            STEP_BUFS,
            pltpu.SemaphoreType.DMA((13,)),
            pltpu.SemaphoreType.DMA((LINKS,)),
            pltpu.SemaphoreType.DMA((LINKS,)),
        ],
        compiler_params=pltpu.CompilerParams(
            collective_id=0, has_side_effects=True, vmem_limit_bytes=56 * 1024 * 1024
        ),
        name="training_step",
    )(
        query_features,
        positive_features,
        negative_features,
        query_first,
        query_second,
        query_third,
        item_first,
        item_second,
        item_third,
        positive_ids.reshape(16, 128),
        positive_counts.reshape(2, 128),
        negative_ids.reshape(16, 128),
        negative_counts.reshape(16, 128),
    )
    *clipped, loss = pl.pallas_call(
        clip_kernel,
        out_shape=tower + tower + (jax.ShapeDtypeStruct((1, 1), F32),),
        in_specs=[vmem] * 7,
        out_specs=(vmem,) * 7,
        name="clip",
    )(scalars, *raw)
    return (loss.reshape(()), *clipped)


def solution(mesh):
    torus = Mesh(mesh.devices.reshape(4, 8, 4, 2), DP_NEG)
    placed = (
        P(DP_NEG, None),
        P(DP_NEG, None),
        P(NEG_DP, None),
        P(DP),
        P(DP_NEG),
        P(NEG),
        P(NEG),
        P(),
        P(),
        P(),
        P(),
        P(),
        P(),
    )
    return jax.shard_map(
        per_device,
        mesh=torus,
        in_specs=placed,
        out_specs=(P(),) + (P(DP, None),) * 6,
        check_vma=False,
    )
```

time: 117 us -> 98 us (0.84)
  Pallas kernels: 108 us -> 97.3 us
  local copies, waits for them, and re-layouts: 4.76 us -> 0 us
  between operations: 2.43 us -> 0.65 us
  other arithmetic: 1.3 us -> 0 us
    pallas_call x1 -> x2, Pallas kernels: 108 us -> 97.3 us  [the longest x1 95.5 us: per_device(): pl.pallas_call(step_kernel, out_shape=tower + tower + (jax.ShapeDtypeStru...]
    squeeze x3 -> x0, local copies, waits for them, and re-layouts: 3.57 us -> none  [the longest x1 1.56 us: per_device(): first[1]]
    convert_element_type x1 -> x0, other arithmetic: 1.3 us -> none  [per_device(): positive_ids.astype(F32).reshape(1, 2048)]
    slice x1 -> x0, local copies, waits for them, and re-layouts: 1.19 us -> none  [per_device(): mean_loss = loss[0, 0] / queries]
where the time goes in v3:
time: 98 us; the launch traced here: 97.9 us
  Pallas kernels  97.3 us (99%)
    pallas_call x1, Pallas kernels, per_device(): pl.pallas_call(step_kernel, out_shape=tower + tower + (jax.ShapeDtypeStru...  95.5 us

profile of v3, /device:TPU:1, one launch (start us, length us, event | category | flops | bytes accessed | tf_op | source)
XLA Modules:
  0.0 97.9 jit_solution(16894615057028338038)
XLA Ops:
  0.6 95.5 %training_step.1 = (f32[16,1024]{1,0:T(8,128)}, f32[32,512]{1,0:T(8,128)}, f32[16,256]{1,0:T(8,128)}, f32[16,1024]{1,0:T(8,128)}, f32[32,512]{1,0:T(8,128)}, /*index=5*/f32[16,256]{1,0:T(8,128)}, f32[2,8,128]{2,1,0:T(8,128)}) custom-call(bf16[256,512]{1,0:T(8,128)(2,1)} %query_x.1, bf16[256,512]{1,0:T(8,128)(2,1)} %positive_x.1, bf16[64,512]{1,0:T(8,128)(2,1)} %negative_x.1, ...), custom_call_target="tpu_custom_call" | custom-call | tf_op jit(solution)/shard_map/training_step/pallas_call | solution.py:955
  96.2 1.7 %clip.1 = (f32[16,1024]{1,0:T(8,128)}, f32[32,512]{1,0:T(8,128)}, f32[16,256]{1,0:T(8,128)}, f32[16,1024]{1,0:T(8,128)}, f32[32,512]{1,0:T(8,128)}, /*index=5*/f32[16,256]{1,0:T(8,128)}, f32[1,1]{1,0:T(1,128)}) custom-call(f32[2,8,128]{2,1,0:T(8,128)} %get-tuple-element.21.refs_0_, f32[16,1024]{1,0:T(8,128)} %get-tuple-element.22.refs_1_, ...), custom_call_target="tpu_custom_call" | custom-call | tf_op jit(solution)/shard_map/clip/pallas_call | solution.py:985

commit v4 on v3

--- a/solution.py
+++ b/solution.py
@@ -235,15 +235,11 @@
         b, links = self.b, self.links
         fx_sum, sy_sum = b["fx_sum"], b["sy_sum"]
         self.first_x.end(fx_sum)
-        self.first_y = Ring4(
-            links, AX_Y, lambda j: fx_sum.at[pl.ds(multiple(j, 8), 8)], 8, b["fy"], 4
-        )
-        self.first_y.start()
+        self.first_y = Direct(links, AX_Y, 4, b["fy"])
+        self.first_y.start(lambda j: fx_sum.at[pl.ds(multiple(j, 8), 8)])
         self.second_y.end(sy_sum)
-        self.second_x = Ring4(
-            links, AX_X, lambda j: sy_sum.at[:, :, pl.ds(multiple(j, 128), 128)], 8, b["sx"], 4
-        )
-        self.second_x.start()
+        self.second_x = Direct(links, AX_X, 4, b["sx"])
+        self.second_x.start(lambda j: sy_sum.at[:, :, pl.ds(multiple(j, 128), 128)])
 
     def third3(self):
         b = self.b
@@ -253,15 +249,17 @@
         self.third_x = Direct(self.links, AX_X, 4, b["tx"])
         self.third_x.start(lambda j: b["ty_sum"])
 
-    def relay2(self):
-        self.first_y.relay()
-        self.second_x.relay()
-
     def stage3(self):
         b = self.b
         both = b["both"]
-        self.first_y.end(both.at[:, 0])
-        self.second_x.end(both.at[:, 1])
+        self.first_y.wait()
+        own = b["fx_sum"].at[pl.ds(multiple(self.y, 8), 8)]
+        slots = [b["fy"].at[lax.rem(self.y + k, 4)] for k in range(1, 4)]
+        add_rows(both.at[:, 0], [own] + slots, 8, 8)
+        self.second_x.wait()
+        own = b["sy_sum"].at[:, :, pl.ds(multiple(self.x, 128), 128)]
+        slots = [b["sx"].at[lax.rem(self.x + k, 4)] for k in range(1, 4)]
+        add_rows(both.at[:, 1], [own] + slots, 8, 8)
         self.last_z = Direct(self.links, AX_Z, 8, b["lz"])
         self.last_z.start(lambda j: both.at[j])
 
@@ -320,8 +318,8 @@
     "tx": pltpu.VMEM((4, 16, 128), BF16),
     "fx_sum": pltpu.VMEM((32, 16, 128), BF16),
     "sy_sum": pltpu.VMEM((8, 16, 512), BF16),
-    "fy": ring_land(8, 16, 128),
-    "sx": ring_land(8, 16, 128),
+    "fy": pltpu.VMEM((4, 8, 16, 128), BF16),
+    "sx": pltpu.VMEM((4, 8, 16, 128), BF16),
     "both": pltpu.VMEM((8, 2, 16, 128), BF16),
     "lz": pltpu.VMEM((8, 2, 16, 128), BF16),
     "own": pltpu.VMEM((2, 16, 128), F32),
@@ -412,9 +410,9 @@
     "p_ring": ring_land(256, 256),
     "p_sum": pltpu.VMEM((256, 256), F32),
     "g_out": pltpu.VMEM((2048, 256), BF16),
-    "g_ring": ring_land(512, 256),
-    "g_sum": pltpu.VMEM((512, 256), BF16),
-    "g_z": pltpu.VMEM((8, 64, 256), BF16),
+    "g_ring": (ring_land(512, 128), ring_land(512, 128)),
+    "g_sum": pltpu.VMEM((2, 512, 128), BF16),
+    "g_z": pltpu.VMEM((2, 8, 64, 128), BF16),
     "g_first": pltpu.VMEM((2, 32, 16, 1024), BF16),
     "g_second": pltpu.VMEM((2, 32, 2, 16, 512), BF16),
     "g_third": pltpu.VMEM((2, 4, 8, 16, 256), BF16),
@@ -446,7 +444,7 @@
         b["s1"][rows, cols] = slope
         return carry
 
-    lax.fori_loop(0, 2, layer, 0)
+    lax.fori_loop(0, 2, layer, 0, unroll=True)
     for made in loads:
         made.wait()
     act, slope = silu_both(dot(b["a1"][rows, :], b["w2"][t]))
@@ -473,7 +471,7 @@
         b["d1"][rows, cols] = slope.astype(BF16)
         return carry
 
-    lax.fori_loop(0, 2, layer, 0)
+    lax.fori_loop(0, 2, layer, 0, unroll=True)
 
 
 def weight_gradients(b, t, rows, tower):
@@ -483,7 +481,7 @@
         b["g_first"][t, :, :, cols] = made.reshape(32, 16, 512)
         return carry
 
-    lax.fori_loop(0, 2, first, 0)
+    lax.fori_loop(0, 2, first, 0, unroll=True)
     tower.pair_first()
 
     def second(i, carry):
@@ -492,7 +490,7 @@
         b["g_second"][t, pl.ds(multiple(i, 16), 16)] = made.reshape(16, 2, 16, 512)
         return carry
 
-    lax.fori_loop(0, 2, second, 0)
+    lax.fori_loop(0, 2, second, 0, unroll=True)
     tower.pair_second()
     third = dot(b["a2t"][:, rows], b["eg"][rows, :]).astype(BF16)
     b["g_third"][t] = third.reshape(4, 8, 16, 256)
@@ -508,7 +506,7 @@
             b[name + "t"][at, rows] = turned.astype(BF16)
             return carry
 
-        lax.fori_loop(0, cols // 256, block, 0)
+        lax.fori_loop(0, cols // 256, block, 0, unroll=True)
 
 
 def column(row):
@@ -561,10 +559,8 @@
 ):
     y, z, x, c = (lax.axis_index(a) for a in (AX_Y, AX_Z, AX_X, AX_C))
     me = x * 2 + c
-    barrier, peers = greet_neighbours()
     links = Links(send, recv, LINKS)
     phase = Phases()
-    phase("load")
 
     loads = [
         (negative_x, b["x"].at[pl.ds(512, 64)]),
@@ -582,7 +578,11 @@
         (neg_counts_in, b["neg_counts"]),
     ]
     loads = [pltpu.make_async_copy(s, d, load.at[k]) for k, (s, d) in enumerate(loads)]
-    for made in loads:
+    for made in loads[:4]:
+        made.start()
+    barrier, peers = greet_neighbours()
+    phase("load")
+    for made in loads[4:]:
         made.start()
 
     b["x"][pl.ds(576, 64), :] = jnp.zeros((64, 512), BF16)
@@ -639,8 +639,10 @@
     q[pl.ds(multiple(me, 256), 256), :] = q_own
     x_up, x_down, x_far = lax.rem(x + 1, 4), lax.rem(x + 3, 4), lax.rem(x + 2, 4)
     other = {AX_C: 1 - c}
-    q_up = links.copy(q_block(x, c), q_block(x, c), {AX_X: x_up})
-    q_down = links.copy(q_block(x, c), q_block(x, c), {AX_X: x_down})
+    q_up, q_down = {}, {}
+    for h in range(2):
+        q_up[h] = links.copy(q_half(x, c, h), q_half(x, c, h), {AX_X: x_up})
+        q_down[1 - h] = links.copy(q_half(x, c, 1 - h), q_half(x, c, 1 - h), {AX_X: x_down})
     q_pair = [links.copy(q_block(x, c), q_block(x, c), other)]
 
     phase("f_pos")
@@ -656,11 +658,13 @@
         n_z[k].wait_recv()
         n_forward(k)
     phase("q_relay")
-    q_up.wait_recv()
+    q_up[0].wait_recv()
     q_low = links.copy(q_half(x_down, c, 0), q_half(x_down, c, 0), {AX_X: x_up})
+    q_down[1].wait_recv()
+    q_high = links.copy(q_half(x_up, c, 1), q_half(x_up, c, 1), {AX_X: x_down})
+    q_up[1].wait_recv()
     q_pair.append(links.copy(q_block(x_down, c), q_block(x_down, c), other))
-    q_down.wait_recv()
-    q_high = links.copy(q_half(x_up, c, 1), q_half(x_up, c, 1), {AX_X: x_down})
+    q_down[0].wait_recv()
     q_pair.append(links.copy(q_block(x_up, c), q_block(x_up, c), other))
 
     phase("small")
@@ -744,7 +748,7 @@
         score_tile(b, pos_ids, y_far, i)
         return carry
 
-    lax.fori_loop(0, 4, far_tiles, 0)
+    lax.fori_loop(0, 4, far_tiles, 0, unroll=2)
 
     phase("den")
     den_out, den_in = b["den_out"], b["den_in"]
@@ -760,7 +764,7 @@
         turn_negatives(b, u)
         return carry
 
-    lax.fori_loop(0, 4, turned, 0)
+    lax.fori_loop(0, 4, turned, 0, unroll=True)
 
     phase("p_theirs")
     p_out = b["p_out"]
@@ -777,11 +781,11 @@
         query_block(c, i)
         return carry
 
-    lax.fori_loop(0, 4, theirs, 0)
+    lax.fori_loop(0, 4, theirs, 0, unroll=2)
     p_pair = b["p_pair"]
     pair = links.copy(p_out.at[1 - c], p_pair, other)
     phase("p_ours")
-    lax.fori_loop(0, 4, ours, 0)
+    lax.fori_loop(0, 4, ours, 0, unroll=2)
     phase("p_add")
     pair.wait_recv()
     for i in range(4):
@@ -807,16 +811,32 @@
         at = pl.ds(multiple(u, 512), 512)
         g_out[at, :] = dot(b["et"][at, :], b["qs"][...]).astype(BF16)
 
-    g_y = Ring4(links, AX_Y, lambda j: g_out.at[pl.ds(multiple(j, 512), 512)], 512, b["g_ring"], 64)
-    negative_rows(g_y.far)
-    g_y.start_far()
-    negative_rows(g_y.up)
-    negative_rows(g_y.down)
-    g_y.start_near()
+    g_y, g_z, g_sum = [], [], b["g_sum"]
+    for h in range(2):
+        cols = pl.ds(h * 128, 128)
+
+        def cut(j, cols=cols):
+            return g_out.at[pl.ds(multiple(j, 512), 512), cols]
+
+        g_y.append(Ring4(links, AX_Y, cut, 512, b["g_ring"][h], 64))
+        g_z.append(Direct(links, AX_Z, 8, b["g_z"].at[h]))
+    negative_rows(g_y[0].far)
+    g_y[0].start_far()
+    g_y[1].start_far()
+    negative_rows(g_y[0].up)
+    negative_rows(g_y[0].down)
+    g_y[0].start_near()
+
+    def g_line(h):
+        g_y[h].end(g_sum.at[h])
+        g_z[h].start(lambda j: g_sum.at[h, pl.ds(multiple(j, 64), 64)])
     phase("p_relay")
     p_x.relay()
     phase("g_own")
-    negative_rows(g_y.me)
+    negative_rows(g_y[0].me)
+    phase("g_relay0")
+    g_y[0].relay()
+    g_y[1].start_near()
 
     phase("slopes")
     losses, slopes, scales = [], [], []
@@ -834,8 +854,8 @@
     phase("b_pos")
     own = q[pl.ds(multiple(me, 256), 256), :].astype(F32)
     backward(b, 1, P_ROWS, slopes * own)
-    phase("g_relay")
-    g_y.relay()
+    phase("g_relay1")
+    g_y[1].relay()
     phase("turn_q")
     turn_activations(b, Q_ROWS)
 
@@ -844,69 +864,67 @@
     query_grad = b["p_sum"][...].T * scales + slopes * b["pos"][...].astype(F32)
     phase("b_query")
     backward(b, 0, Q_ROWS, query_grad)
+    phase("g_end0")
+    g_line(0)
     phase("w_query")
     query_sum = TowerSum(links, b["sum_query"], b, 0)
     item_sum = TowerSum(links, b["sum_item"], b, 1)
     weight_gradients(b, 0, Q_ROWS, query_sum)
-    phase("g_end")
-    g_sum = b["g_sum"]
-    g_y.end(g_sum)
-    g_z = Direct(links, AX_Z, 8, b["g_z"])
-    g_z.start(lambda j: g_sum.at[pl.ds(multiple(j, 64), 64)])
-
+    phase("g_end1")
+    g_line(1)
+
+    phase("turn_n")
+    turn_activations(b, N_ROWS)
     phase("q_stage1")
     query_sum.stage1()
     phase("turn_p")
     turn_activations(b, P_ROWS)
     phase("q_relay1")
     query_sum.relay1()
-    phase("turn_n")
-    turn_activations(b, N_ROWS)
 
     phase("g_z")
-    g_z.wait()
-    total = g_sum[pl.ds(multiple(z, 64), 64), :].astype(F32)
-    for k in range(1, 8):
-        total = total + b["g_z"][lax.rem(z + k, 8)].astype(F32)
+    halves = []
+    for h in range(2):
+        g_z[h].wait()
+        total = g_sum[h, pl.ds(multiple(z, 64), 64), :].astype(F32)
+        for k in range(1, 8):
+            total = total + b["g_z"][h, lax.rem(z + k, 8)].astype(F32)
+        halves.append(total)
+    total = jnp.concatenate(halves, axis=1)
     total = jnp.concatenate([total * inv_temp, jnp.zeros((64, 256), F32)], axis=0)
     phase("b_neg")
     backward(b, 1, N_ROWS, total)
+    phase("w_item")
+    weight_gradients(b, 1, I_ROWS, item_sum)
+    phase("i_stage1")
+    item_sum.stage1()
     phase("q_stage2")
     query_sum.stage2()
     query_sum.third1()
-    phase("w_item")
-    weight_gradients(b, 1, I_ROWS, item_sum)
-    phase("q_relay2")
-    query_sum.relay2()
-    phase("i_stage1")
-    item_sum.stage1()
     item_sum.third1()
-    phase("q_third2")
-    query_sum.third2()
+    phase("i_relay1")
+    item_sum.relay1()
     phase("q_stage3")
     query_sum.stage3()
-    phase("i_relay1")
-    item_sum.relay1()
+    query_sum.third2()
     phase("i_stage2")
     item_sum.stage2()
     phase("q_third3")
     query_sum.third3()
     item_sum.third2()
-    phase("i_relay2")
-    item_sum.relay2()
+    phase("i_stage3")
+    item_sum.stage3()
+    phase("q_last")
     item_sum.third3()
-    phase("q_last")
     squares = query_sum.last()
     query_sum.spread()
-    phase("i_stage3")
-    item_sum.stage3()
     phase("i_last")
     squares = squares + item_sum.last()
     scalars = Scalars(links, b["scalars"])
     scalars.start(squares)
-    item_sum.spread()
     phase("group")
     scalars.over_plane()
+    item_sum.spread()
     phase("plane")
     total = scalars.end()
     row = lax.broadcasted_iota(jnp.int32, (8, 128), 0)

time: 98 us -> 90.8 us (0.927)
  Pallas kernels: 97.3 us -> 89.9 us
    pallas_call x1, Pallas kernels: 95.5 us -> 88.2 us  [per_device(): pl.pallas_call(step_kernel, out_shape=tower + tower + (jax.ShapeDtypeStru...]
where the time goes in v4:
time: 90.8 us; the launch traced here: 90.6 us
  Pallas kernels  89.9 us (99%)
    pallas_call x1, Pallas kernels, per_device(): pl.pallas_call(step_kernel, out_shape=tower + tower + (jax.ShapeDtypeStru...  88.2 us

profile of v4, /device:TPU:1, one launch (start us, length us, event | category | flops | bytes accessed | tf_op | source)
XLA Modules:
  0.0 90.6 jit_solution(1566216256939250414)
XLA Ops:
  0.6 88.2 %training_step.1 = (f32[16,1024]{1,0:T(8,128)}, f32[32,512]{1,0:T(8,128)}, f32[16,256]{1,0:T(8,128)}, f32[16,1024]{1,0:T(8,128)}, f32[32,512]{1,0:T(8,128)}, /*index=5*/f32[16,256]{1,0:T(8,128)}, f32[2,8,128]{2,1,0:T(8,128)}) custom-call(bf16[256,512]{1,0:T(8,128)(2,1)} %query_x.1, bf16[256,512]{1,0:T(8,128)(2,1)} %positive_x.1, bf16[64,512]{1,0:T(8,128)(2,1)} %negative_x.1, ...), custom_call_target="tpu_custom_call" | custom-call | tf_op jit(solution)/shard_map/training_step/pallas_call | solution.py:973
  88.9 1.7 %clip.1 = (f32[16,1024]{1,0:T(8,128)}, f32[32,512]{1,0:T(8,128)}, f32[16,256]{1,0:T(8,128)}, f32[16,1024]{1,0:T(8,128)}, f32[32,512]{1,0:T(8,128)}, /*index=5*/f32[16,256]{1,0:T(8,128)}, f32[1,1]{1,0:T(1,128)}) custom-call(f32[2,8,128]{2,1,0:T(8,128)} %get-tuple-element.21.refs_0_, f32[16,1024]{1,0:T(8,128)} %get-tuple-element.22.refs_1_, ...), custom_call_target="tpu_custom_call" | custom-call | tf_op jit(solution)/shard_map/clip/pallas_call | solution.py:1003

commit v5 on v4

--- a/solution.py
+++ b/solution.py
@@ -92,9 +92,15 @@
         self.b = self.links.copy(far.at[self.high], self.early_down, {self.axis: self.down})
 
     def start_near(self):
+        self.start_up()
+        self.start_down()
+
+    def start_up(self):
         self.c = self.links.copy(
             self.cut(self.up).at[self.high], self.from_down.at[self.high], {self.axis: self.up}
         )
+
+    def start_down(self):
         self.d = self.links.copy(
             self.cut(self.down).at[self.low], self.from_up.at[self.low], {self.axis: self.down}
         )
@@ -368,7 +374,6 @@
 
 
 Q_ROWS, P_ROWS, N_ROWS = pl.ds(0, 256), pl.ds(256, 256), pl.ds(512, 128)
-I_ROWS = pl.ds(256, 384)
 
 STEP_BUFS = {
     "pos_ids": pltpu.VMEM((16, 128), jnp.int32),
@@ -416,6 +421,10 @@
     "g_first": pltpu.VMEM((2, 32, 16, 1024), BF16),
     "g_second": pltpu.VMEM((2, 32, 2, 16, 512), BF16),
     "g_third": pltpu.VMEM((2, 4, 8, 16, 256), BF16),
+    "kept_first": pltpu.VMEM((512, 1024), F32),
+    "kept_second": pltpu.VMEM((1024, 512), F32),
+    "kept_third": pltpu.VMEM((512, 256), F32),
+    "stage": tuple(pltpu.VMEM(shape, F32) for shape in ((16, 1024), (32, 512), (16, 256)) * 2),
     "sum_query": SUM_BUFS,
     "sum_item": SUM_BUFS,
     "scalars": SCALAR_BUFS,
@@ -474,27 +483,43 @@
     lax.fori_loop(0, 2, layer, 0, unroll=True)
 
 
-def weight_gradients(b, t, rows, tower):
+def weight_gradients(b, t, rows, tower=None, add=False):
+    def store(name, at, shape, value):
+        if add:
+            value = value + b["kept_" + name][at]
+        if tower is None:
+            b["kept_" + name][at] = value
+        elif name == "first":
+            b["g_first"][t, :, :, at[1]] = value.astype(BF16).reshape(shape)
+        elif name == "second":
+            b["g_second"][t, shape[0]] = value.astype(BF16).reshape(shape[1])
+        else:
+            b["g_third"][t] = value.astype(BF16).reshape(shape)
+
     def first(i, carry):
         cols = pl.ds(multiple(i, 512), 512)
-        made = dot(b["xt"][:, rows], b["d1"][rows, cols]).astype(BF16)
-        b["g_first"][t, :, :, cols] = made.reshape(32, 16, 512)
+        made = dot(b["xt"][:, rows], b["d1"][rows, cols])
+        store("first", (slice(None), cols), (32, 16, 512), made)
         return carry
 
     lax.fori_loop(0, 2, first, 0, unroll=True)
-    tower.pair_first()
+    if tower is not None:
+        tower.pair_first()
 
     def second(i, carry):
         at = pl.ds(multiple(i, 512), 512)
-        made = dot(b["a1t"][at, rows], b["d2"][rows, :]).astype(BF16)
-        b["g_second"][t, pl.ds(multiple(i, 16), 16)] = made.reshape(16, 2, 16, 512)
+        made = dot(b["a1t"][at, rows], b["d2"][rows, :])
+        shape = (pl.ds(multiple(i, 16), 16), (16, 2, 16, 512))
+        store("second", (at, slice(None)), shape, made)
         return carry
 
     lax.fori_loop(0, 2, second, 0, unroll=True)
-    tower.pair_second()
-    third = dot(b["a2t"][:, rows], b["eg"][rows, :]).astype(BF16)
-    b["g_third"][t] = third.reshape(4, 8, 16, 256)
-    tower.pair_third()
+    if tower is not None:
+        tower.pair_second()
+    made = dot(b["a2t"][:, rows], b["eg"][rows, :])
+    store("third", (slice(None), slice(None)), (4, 8, 16, 256), made)
+    if tower is not None:
+        tower.pair_third()
 
 
 def turn_activations(b, rows):
@@ -612,8 +637,12 @@
     y_up, y_down = lax.rem(y + 1, 4), lax.rem(y + 3, 4)
     order = (1, 7, 2, 6, 3, 5, 4)
     n_z, n_y = {}, {}
-    for k in order:
-        n_z[k] = links.copy(n_block(y, z), n_block(y, z), {AX_Z: lax.rem(z + k, 8)})
+
+    def n_along(*which):
+        for k in which:
+            n_z[k] = links.copy(n_block(y, z), n_block(y, z), {AX_Z: lax.rem(z + k, 8)})
+
+    n_along(1, 7, 2, 6)
 
     def n_forward(k):
         zz = lax.rem(z - k + 8, 8)
@@ -637,6 +666,7 @@
         return q.at[pl.ds(pl.multiple_of((xx * 2 + cc) * 256 + h * 128, 128), 128)]
 
     q[pl.ds(multiple(me, 256), 256), :] = q_own
+    n_along(3, 5, 4)
     x_up, x_down, x_far = lax.rem(x + 1, 4), lax.rem(x + 3, 4), lax.rem(x + 2, 4)
     other = {AX_C: 1 - c}
     q_up, q_down = {}, {}
@@ -653,7 +683,23 @@
     )
     b["pos"][...] = forward(b, 1, P_ROWS)
 
+    n_far = []
+
+    def n_relay(*which):
+        for k in which:
+            zz = lax.rem(z - k + 8, 8)
+            from_down, from_up = n_y[k]
+            from_down.wait_recv()
+            n_far.append(
+                links.copy(n_half(y_down, zz, 0), n_half(y_down, zz, 0), {AX_Y: y_up})
+            )
+            from_up.wait_recv()
+            n_far.append(
+                links.copy(n_half(y_up, zz, 1), n_half(y_up, zz, 1), {AX_Y: y_down})
+            )
+
     phase("n_fwd1")
+    n_relay(0)
     for k in order[:4]:
         n_z[k].wait_recv()
         n_forward(k)
@@ -683,23 +729,8 @@
         n_z[k].wait_recv()
         n_forward(k)
 
-    n_far = []
-
-    def n_relay(*which):
-        for k in which:
-            zz = lax.rem(z - k + 8, 8)
-            from_down, from_up = n_y[k]
-            from_down.wait_recv()
-            n_far.append(
-                links.copy(n_half(y_down, zz, 0), n_half(y_down, zz, 0), {AX_Y: y_up})
-            )
-            from_up.wait_recv()
-            n_far.append(
-                links.copy(n_half(y_up, zz, 1), n_half(y_up, zz, 1), {AX_Y: y_down})
-            )
-
     phase("relay_a")
-    n_relay(0, 1, 7)
+    n_relay(1, 7)
     q_pair[0].wait_recv()
     phase("tile_a")
     score_tile(b, pos_ids, y, x)
@@ -729,7 +760,7 @@
         score_tile(b, pos_ids, y_down, i)
         return carry
 
-    lax.fori_loop(0, 4, near_tiles, 0)
+    lax.fori_loop(0, 4, near_tiles, 0, unroll=2)
     phase("logits")
     own = b["q"][pl.ds(multiple(me, 256), 256), :].astype(F32)
     along = jnp.sum(own * b["pos"][...].astype(F32), axis=1, keepdims=True)
@@ -748,7 +779,7 @@
         score_tile(b, pos_ids, y_far, i)
         return carry
 
-    lax.fori_loop(0, 4, far_tiles, 0, unroll=2)
+    lax.fori_loop(0, 4, far_tiles, 0, unroll=True)
 
     phase("den")
     den_out, den_in = b["den_out"], b["den_in"]
@@ -879,6 +910,8 @@
     query_sum.stage1()
     phase("turn_p")
     turn_activations(b, P_ROWS)
+    phase("w_pos")
+    weight_gradients(b, 1, P_ROWS)
     phase("q_relay1")
     query_sum.relay1()
 
@@ -895,7 +928,7 @@
     phase("b_neg")
     backward(b, 1, N_ROWS, total)
     phase("w_item")
-    weight_gradients(b, 1, I_ROWS, item_sum)
+    weight_gradients(b, 1, N_ROWS, item_sum, add=True)
     phase("i_stage1")
     item_sum.stage1()
     phase("q_stage2")
@@ -925,6 +958,27 @@
     phase("group")
     scalars.over_plane()
     item_sum.spread()
+    phase("pieces")
+    stage = b["stage"]
+    query_sum.collect(*stage[:3])
+    item_sum.collect(*stage[3:])
+    stores = [
+        pltpu.make_async_copy(stage[k], result, load.at[13 + k])
+        for k, result in enumerate(
+            (
+                o_query_first,
+                o_query_second,
+                o_query_third,
+                o_item_first,
+                o_item_second,
+                o_item_third,
+            )
+        )
+    ]
+    for made in stores:
+        made.start()
+    phase("finish")
+    links.finish()
     phase("plane")
     total = scalars.end()
     row = lax.broadcasted_iota(jnp.int32, (8, 128), 0)
@@ -932,11 +986,8 @@
     factor = clip_norm / jnp.maximum(norm, clip_norm)
     o_scalars[0] = jnp.broadcast_to(factor, (8, 128))
     o_scalars[1] = jnp.broadcast_to(jnp.sum(jnp.where((row == 1) | (row == 2), total, 0.0), keepdims=True), (8, 128))
-    phase("pieces")
-    query_sum.collect(o_query_first, o_query_second, o_query_third)
-    item_sum.collect(o_item_first, o_item_second, o_item_third)
-    phase("finish")
-    links.finish()
+    for made in stores:
+        made.wait()
     phase(None)
 
 
@@ -974,15 +1025,15 @@
         step_kernel,
         out_shape=tower + tower + (jax.ShapeDtypeStruct((2, 8, 128), F32),),
         in_specs=[anywhere] * 13,
-        out_specs=(vmem,) * 7,
+        out_specs=(anywhere,) * 6 + (vmem,),
         scratch_shapes=[
             STEP_BUFS,
-            pltpu.SemaphoreType.DMA((13,)),
+            pltpu.SemaphoreType.DMA((19,)),
             pltpu.SemaphoreType.DMA((LINKS,)),
             pltpu.SemaphoreType.DMA((LINKS,)),
         ],
         compiler_params=pltpu.CompilerParams(
-            collective_id=0, has_side_effects=True, vmem_limit_bytes=56 * 1024 * 1024
+            collective_id=0, has_side_effects=True, vmem_limit_bytes=60 * 1024 * 1024
         ),
         name="training_step",
     )(

time: 90.8 us -> 88.8 us (0.978)
  Pallas kernels: 89.9 us -> 88 us
    pallas_call x1, Pallas kernels: 88.2 us -> 86.2 us  [per_device(): pl.pallas_call(step_kernel, out_shape=tower + tower + (jax.ShapeDtypeStru...]
where the time goes in v5:
time: 88.8 us; the launch traced here: 88.6 us
  Pallas kernels  88 us (99%)
    pallas_call x1, Pallas kernels, per_device(): pl.pallas_call(step_kernel, out_shape=tower + tower + (jax.ShapeDtypeStru...  86.2 us

profile of v5, /device:TPU:1, one launch (start us, length us, event | category | flops | bytes accessed | tf_op | source)
XLA Modules:
  0.0 88.6 jit_solution(12181982561125977507)
XLA Ops:
  0.6 86.2 %training_step.1 = (f32[16,1024]{1,0:T(8,128)}, f32[32,512]{1,0:T(8,128)}, f32[16,256]{1,0:T(8,128)}, f32[16,1024]{1,0:T(8,128)}, f32[32,512]{1,0:T(8,128)}, /*index=5*/f32[16,256]{1,0:T(8,128)}, f32[2,8,128]{2,1,0:T(8,128)}) custom-call(bf16[256,512]{1,0:T(8,128)(2,1)} %query_x.1, bf16[256,512]{1,0:T(8,128)(2,1)} %positive_x.1, bf16[64,512]{1,0:T(8,128)(2,1)} %negative_x.1, ...), custom_call_target="tpu_custom_call" | custom-call | tf_op jit(solution)/shard_map/training_step/pallas_call | solution.py:1024
  86.9 1.7 %clip.1 = (f32[16,1024]{1,0:T(8,128)}, f32[32,512]{1,0:T(8,128)}, f32[16,256]{1,0:T(8,128)}, f32[16,1024]{1,0:T(8,128)}, f32[32,512]{1,0:T(8,128)}, /*index=5*/f32[16,256]{1,0:T(8,128)}, f32[1,1]{1,0:T(1,128)}) custom-call(f32[2,8,128]{2,1,0:T(8,128)} %get-tuple-element.21.refs_0_, f32[16,1024]{1,0:T(8,128)} %get-tuple-element.22.refs_1_, ...), custom_call_target="tpu_custom_call" | custom-call | tf_op jit(solution)/shard_map/clip/pallas_call | solution.py:1054
